TPU v7x, 256 devices: a whole 4x4x8 slice. The times are simulated.
256 devices in a mesh: horizon: 32 (over z, x), batch: 8 (over y, core).
Axes of the slice: x: 4, y: 4, z: 8, core: 2. Of those that a mesh axis runs over, the one named last changes fastest.
Arguments:
- dynamics: float32 [8, 256, 48, 48], P('batch', 'horizon'), may hold values from -0.1 to 1.1
- inputs: float32 [8, 256, 48, 16], P('batch', 'horizon'), may hold values from -0.6 to 0.6
- state_cost: float32 [8, 256, 48, 48], P('batch', 'horizon'), may hold values from -1 to 1, as said below
- input_cost: float32 [8, 256, 16, 16], P('batch', 'horizon'), may hold values from -0.2 to 2.2, as said below
- drift: float32 [8, 256, 48], P('batch', 'horizon'), may hold values from -0.6 to 0.6
- target: float32 [8, 256, 48], P('batch', 'horizon'), may hold values from -6 to 6
- initial: float32 [8, 48], P('batch'), may hold values from -6 to 6
Outputs:
- hessian: float32 [8, 4096, 4096], P('batch', 'horizon')
- gradient: float32 [8, 4096], P('batch', 'horizon')
Inputs may be any that keep to these rules, and one draw needn't show every extreme that they name: `state_cost`: each 48 x 48 matrix is symmetric and positive definite. `input_cost`: each 16 x 16 matrix is symmetric and positive definite.
All inputs are finite; a program needn't handle non-finite values.
Results may differ from a plain program's by a relative error of at most 0.0003.
Values sent between devices are 32-bit elements; how exact they have to be, the bound alone decides.
A program may use at most 128 MiB of HBM per device.

v0:
```python
import jax
import jax.numpy as jnp
from jax import lax
from jax.sharding import Mesh
from jax.sharding import PartitionSpec as P

NX = 48
NU = 16
HORIZON = ("horizon_0", "horizon_1")


HI = lax.Precision.HIGHEST


def copy_for_each(array, axis):
    copies = jnp.broadcast_to(array, (lax.axis_size(axis), *array.shape))
    return lax.all_to_all(copies, axis, split_axis=0, concat_axis=0, tiled=True)


def all_in_one(array, axis):
    leaves = jax.tree.leaves(array)
    sequence = sorted(range(len(leaves)), key=lambda k: -leaves[k].size)
    width = (1, *leaves[sequence[0]].shape)[-1]
    lines = [
        jnp.pad(leaves[k].reshape(-1), (0, -leaves[k].size % width)).reshape(-1, width)
        for k in sequence
    ]
    both, at, found = (copy_for_each(jnp.concatenate(lines), axis), 0, {})
    for k, line in zip(sequence, lines):
        piece = both[:, at : at + len(line)].reshape(len(both), -1)
        found[k] = piece[:, : leaves[k].size].reshape(-1, *leaves[k].shape)
        at += len(line)
    numbers = iter(range(len(leaves)))
    return jax.tree.map(lambda _: found[next(numbers)], array)


def combined_pairwise(pieces, combine):
    while len(jax.tree.leaves(pieces)[0]) > 1:
        pieces = jax.vmap(combine)(
            *(jax.tree.map(lambda part: part[side::2], pieces) for side in (0, 1))
        )
    return jax.tree.map(lambda part: part[0], pieces)


def prefix(array, axis, combine, identity):
    count, mine = (lax.axis_size(axis), lax.axis_index(axis))
    passed = jnp.arange(count) < mine

    def kept(part, zero, own):
        part = jnp.where(
            passed.reshape(-1, *(1 for _ in own.shape)), part, jnp.asarray(zero, own.dtype)
        )
        return part

    pieces = all_in_one(array, axis)
    return combined_pairwise(jax.tree.map(kept, pieces, identity, array), combine)


def nothing_yet(array, identity):
    return jax.tree.map(
        lambda a, e: jnp.broadcast_to(jnp.asarray(e, a.dtype), a.shape), array, identity
    )


def collected_together(array, axis):
    leaves = jax.tree.leaves(array)
    sequence = sorted(range(len(leaves)), key=lambda k: -leaves[k].size)
    width = (1, *leaves[sequence[0]].shape)[-1]
    lines = [
        jnp.pad(leaves[k].reshape(-1), (0, -leaves[k].size % width)).reshape(-1, width)
        for k in sequence
    ]
    both, at, found = (lax.all_gather(jnp.concatenate(lines), axis), 0, {})
    for k, line in zip(sequence, lines):
        piece = both[:, at : at + len(line)].reshape(len(both), -1)
        found[k] = piece[:, : leaves[k].size].reshape(-1, *leaves[k].shape)
        at += len(line)
    numbers = iter(range(len(leaves)))
    return jax.tree.map(lambda _: found[next(numbers)], array)


def entering(array, axes, combine, identity):
    before = start = nothing_yet(array, identity)
    subtotal = array
    for axis in reversed(axes):
        count, mine = (lax.axis_size(axis), lax.axis_index(axis))
        pieces = collected_together(subtotal, axis)
        inside, subtotal = (start, start)
        for k in reversed(range(count)):
            passed = k > mine
            subtotal = combine(subtotal, jax.tree.map(lambda part: part[k], pieces))
            inside = jax.tree.map(lambda new, old: jnp.where(passed, new, old), subtotal, inside)
        before = combine(inside, before)
    return before


def prefix_by_axis(array, axes, combine, identity):
    before = start = nothing_yet(array, identity)
    subtotal = array
    for axis in reversed(axes):
        count, mine = (lax.axis_size(axis), lax.axis_index(axis))
        pieces = jax.tree.map(lambda part: lax.all_gather(part, axis), subtotal)
        inside, subtotal = (start, start)
        for k in reversed(range(count)):
            passed = k > mine
            subtotal = combine(subtotal, jax.tree.map(lambda part: part[k], pieces))
            inside = jax.tree.map(lambda new, old: jnp.where(passed, new, old), subtotal, inside)
        before = combine(inside, before)
    return before


def times_mat(left, right):
    return jnp.einsum("pij,pjk->pik", left, right, precision=HI)


def trans_mat(left, right):
    return jnp.einsum("pji,pjk->pik", left, right, precision=HI)


def times_vec(left, vector):
    return jnp.einsum("pij,pj->pi", left, vector, precision=HI)


def trans_vec(left, vector):
    return jnp.einsum("pji,pj->pi", left, vector, precision=HI)


def body(dynamics, inputs, state_cost, input_cost, drift, target, initial):
    count = lax.axis_size(HORIZON)
    device = lax.axis_index(HORIZON)
    problems = inputs.shape[0]
    sections = inputs.shape[1]
    local_cols = sections * NU
    total_cols = local_cols * count
    offset_cols = device * local_cols
    eye_state = jnp.broadcast_to(jnp.eye(NX, dtype=jnp.float32), (problems, NX, NX))
    zero_square = jnp.zeros((problems, NX, NX), jnp.float32)
    zero_vector = jnp.zeros((problems, NX), jnp.float32)
    section_dynamics = jnp.moveaxis(dynamics, 1, 0)
    section_inputs = jnp.moveaxis(inputs, 1, 0)
    section_costs = jnp.moveaxis(state_cost, 1, 0)
    section_input_costs = jnp.moveaxis(input_cost, 1, 0)
    section_drift = jnp.moveaxis(drift, 1, 0)
    section_target = jnp.moveaxis(target, 1, 0)
    indices = jnp.arange(sections, dtype=jnp.int32)

    def forward_local(carry, parts):
        transfer, shift_sum = carry
        matrix, shift_vec = parts
        return ((times_mat(matrix, transfer), times_vec(matrix, shift_sum) + shift_vec), None)

    (transfer, shift_sum), _ = lax.scan(
        forward_local, (eye_state, zero_vector), (section_dynamics, section_drift)
    )

    def closing_local(tail, parts):
        matrix, weight = parts
        return (trans_mat(matrix, times_mat(weight + tail, matrix)), None)

    closing, _ = lax.scan(
        closing_local, zero_square, (section_dynamics, section_costs), reverse=True
    )

    def chain_forward(earlier, later):
        return (times_mat(later[0], earlier[0]), times_vec(later[0], earlier[1]) + later[1])

    entry_map, entry_shift = prefix(
        (transfer, shift_sum), HORIZON, chain_forward, (eye_state, zero_vector)
    )

    def chain_backward(earlier, later):
        return (
            times_mat(earlier[0], later[0]),
            trans_mat(later[0], times_mat(earlier[1], later[0])) + later[1],
        )

    _, tail_cost = entering((transfer, closing), HORIZON, chain_backward, (eye_state, zero_square))
    start_state = times_vec(entry_map, initial) + entry_shift

    def roll_states(state, parts):
        matrix, shift_vec, goal, weight = parts
        after = times_vec(matrix, state) + shift_vec
        return (after, times_vec(weight, after - goal))

    _, weighted = lax.scan(
        roll_states, start_state, (section_dynamics, section_drift, section_target, section_costs)
    )

    def sweep_costs(tail, parts):
        matrix, weight = parts
        total_cost = weight + tail
        return (trans_mat(matrix, times_mat(total_cost, matrix)), total_cost)

    _, cost_to_go = lax.scan(
        sweep_costs, tail_cost, (section_dynamics, section_costs), reverse=True
    )
    value_cols = jnp.einsum("spij,spjk->spik", cost_to_go, section_inputs, precision=HI)

    def sweep_compact(carry, parts):
        block, vector = carry
        matrix, value, weight, index = parts
        placed = lax.dynamic_update_slice_in_dim(block, value, index * NU, 2)
        return ((trans_mat(matrix, placed), trans_vec(matrix, weight + vector)), (block, vector))

    compact_start = (jnp.zeros((problems, NX, local_cols), jnp.float32), zero_vector)
    (local_block, local_vector), (later_blocks, later_vectors) = lax.scan(
        sweep_compact,
        compact_start,
        (section_dynamics, value_cols, weighted, indices),
        reverse=True,
    )
    padded = lax.dynamic_update_slice_in_dim(
        jnp.zeros((problems, NX, total_cols), jnp.float32), local_block, offset_cols, 2
    )

    def join_columns(earlier, later):
        return (
            times_mat(earlier[0], later[0]),
            later[1] + trans_mat(later[0], earlier[1]),
            later[2] + trans_vec(later[0], earlier[2]),
        )

    scan_start = (eye_state, jnp.zeros((problems, NX, total_cols), jnp.float32), zero_vector)
    _, incoming, incoming_vec = prefix_by_axis(
        (transfer, padded, local_vector), HORIZON, join_columns, scan_start
    )

    def sweep_rows(carry, parts):
        block, vector = carry
        matrix, control, later_block, later_vector, weight = parts
        row_block = trans_mat(control, block)
        row_block = lax.dynamic_update_slice_in_dim(
            row_block, trans_mat(control, later_block), offset_cols, 2
        )
        grad_block = trans_vec(control, weight + later_vector + vector)
        return ((trans_mat(matrix, block), trans_vec(matrix, vector)), (row_block, grad_block))

    _, (row_blocks, grad_blocks) = lax.scan(
        sweep_rows,
        (incoming, incoming_vec),
        (section_dynamics, section_inputs, later_blocks, later_vectors, weighted),
        reverse=True,
    )
    upper = jnp.moveaxis(row_blocks, 0, 1).reshape(problems, local_cols, total_cols)
    gradient = jnp.moveaxis(grad_blocks, 0, 1).reshape(problems, local_cols)
    received = lax.all_to_all(upper, HORIZON, split_axis=2, concat_axis=2, tiled=True)
    mirrored = jnp.transpose(
        received.reshape(problems, local_cols, count, local_cols), (0, 3, 2, 1)
    ).reshape(problems, local_cols, total_cols)
    diagonal_blocks = (
        jnp.einsum("spji,spjk->spik", section_inputs, value_cols, precision=HI)
        + section_input_costs
    )
    block_diag = jnp.einsum(
        "st,spij->psitj", jnp.eye(sections, dtype=jnp.float32), diagonal_blocks, precision=HI
    ).reshape(problems, local_cols, local_cols)
    hessian = upper + mirrored
    own_tile = lax.dynamic_slice_in_dim(hessian, offset_cols, local_cols, 2) + block_diag
    hessian = lax.dynamic_update_slice_in_dim(hessian, own_tile, offset_cols, 2)
    return (hessian, gradient)


def solution(mesh):
    split = Mesh(
        mesh.devices.reshape(8, 4, mesh.shape["batch"]), ("horizon_0", "horizon_1", "batch")
    )
    return jax.shard_map(
        body,
        mesh=split,
        in_specs=(
            P("batch", HORIZON, None, None),
            P("batch", HORIZON, None, None),
            P("batch", HORIZON, None, None),
            P("batch", HORIZON, None, None),
            P("batch", HORIZON, None),
            P("batch", HORIZON, None),
            P("batch", None),
        ),
        out_specs=(P("batch", HORIZON, None), P("batch", HORIZON)),
        check_vma=False,
    )
```

profile of v0, /device:TPU:8, one launch (start us, length us, event | category | flops | bytes accessed | tf_op | source)
XLA Modules:
  0.0 362.3 jit_solution(9857673720748653147)
XLA Ops:
  7.2 14.7 %while.94 = (s32[]{:T(128)}, f32[1,48,48]{2,1,0:T(8,128)S(1)}, f32[1,48]{1,0:T(1,128)S(1)}, f32[8,1,48,48]{3,2,1,0:T(8,128)}, f32[8,1,48]{2,1,0:T(1,128)}, /*index=5*/s32[]{:T(128)}) while((s32[]{:T(128)}, f32[1,48,48]{2,1,0:T(8,128)S(1)}, f32[1,48]{1,0:T(1,128)S(1)}, f32[8,1,48,48]{3,2,1,0:T(8,128)}, f32[8,1,48]{2,1,0:T(1,128)}, ...), condition=%wide.region_1.2_spmd, body=%wide.region_0.1_spmd.sunk | while | flops 1354802 | bytes 88401 | solution.py:152
  7.2 0.9 fusion.353
  8.2 0.9 convolution_bitcast_fusion.37
  9.1 0.9 fusion.353
  10.0 0.9 convolution_bitcast_fusion.37
  10.9 0.9 fusion.353
  11.8 0.9 convolution_bitcast_fusion.37
  12.8 0.9 fusion.353
  13.7 0.9 convolution_bitcast_fusion.37
  14.6 0.9 fusion.353
  15.5 0.9 convolution_bitcast_fusion.37
  16.5 0.9 fusion.353
  17.3 0.9 convolution_bitcast_fusion.37
  19.2 0.9 convolution_bitcast_fusion.37
  21.0 0.9 convolution_bitcast_fusion.37
  22.3 1.5 reshape.1195
  23.8 11.3 %all-to-all-start = ((f32[32,1,2352]{2,1,0:T(1,128)}), f32[32,1,2352]{2,1,0:T(1,128)S(1)}, u32[]{:S(2)}, u32[]{:S(2)}) async-start(f32[32,1,2352]{2,1,0:T(1,128)} %reshape.1195), calls=%async_computation | async-start | bytes 622592 | tf_op jit(solution)/shard_map/all_to_all | solution.py:17
  35.2 3.3 while.95
  38.7 12.5 %all-gather.7 = f32[4,96,48]{1,2,0:T(8,128)S(1)} all-gather(f32[1,96,48]{1,2,0:T(8,128)S(1)} %maximum_bitcast_fusion.1), channel_id=2, replica_groups=mesh['horizon_0'=8,'horizon_1'=4,'batch'=8] {'horizon_1'}, dimensions={0}, use_global_device_ids=true | all-gather | bytes 92160 | tf_op jit(solution)/shard_map/all_gather | solution.py:73
  54.0 25.7 %all-gather.8 = f32[8,96,48]{1,2,0:T(8,128)S(1)} all-gather(f32[1,96,48]{1,2,0:T(8,128)S(1)} %copy.54), channel_id=3, replica_groups=mesh['horizon_0'=8,'horizon_1'=4,'batch'=8] {'horizon_0'}, dimensions={0}, use_global_device_ids=true | all-gather | bytes 165888 | tf_op jit(solution)/shard_map/all_gather | solution.py:73
  83.8 3.4 while.96
  88.2 1.4 reduce.4
  94.8 13.2 %while.97 = (s32[]{:T(128)}, f32[1,48]{1,0:T(1,128)S(1)}, f32[8,1,48]{2,1,0:T(1,128)S(1)}, f32[8,1,48,48]{3,2,1,0:T(8,128)S(1)}, f32[8,1,48]{2,1,0:T(1,128)}, /*...) while((s32[]{:T(128)}, f32[1,48]{1,0:T(1,128)S(1)}, f32[8,1,48]{2,1,0:T(1,128)S(1)}, ...), condition=%wide.region_7.8_spmd, body=%wide.region_6.7_spmd.sunk | while | flops 55394 | bytes 54621 | solution.py:185
  108.0 17.7 %while.98 = (s32[]{:T(128)}, f32[1,48,128]{2,1,0:T(8,128)S(1)}, f32[1,48]{1,0:T(1,128)S(1)}, f32[8,1,48,128]{3,2,1,0:T(8,128)S(1)}, f32[8,1,48]{2,1,0:T(1,128)S(...) while((s32[]{:T(128)}, f32[1,48,128]{2,1,0:T(8,128)S(1)}, ...), condition=%wide.region_9.10_spmd, body=%wide.region_8.9_spmd.sunk | while | flops 3566647 | bytes 218911 | solution.py:206
  127.4 12.1 %all-gather.2 = f32[4,48,48]{2,1,0:T(8,128)S(1)} all-gather(f32[1,48,48]{2,1,0:T(8,128)S(1)} %get-tuple-element.658), channel_id=4, replica_groups=mesh['horizon_0'=8,'horizon_1'=4,'batch'=8] {'horizon_1'}, dimensions={0}, use_global_device_ids=true | all-gather | bytes 46080 | tf_op jit(solution)/shard_map/all_gather | solution.py:102
  139.5 29.5 %all-gather.13.cloned.1.call-done = f32[4,1,48,4096]{3,2,1,0:T(8,128)} async-done(((f32[1,1,48,4096]{3,2,1,0:T(8,128)}), f32[4,1,48,4096]{3,2,1,0:T(8,128)}) %all-gather.13.cloned.1.call-update) | async-done | bytes 3145744 | tf_op jit(solution)/shard_map/all_gather | solution.py:102
  169.0 1.8 convolution_add_fusion.12
  170.8 2.0 convolution_add_fusion.11
  173.7 1.7 convolution_add_fusion.9
  177.3 27.1 %all-gather.4 = f32[384,48]{1,0:T(8,128)S(1)} all-gather(f32[48,48]{1,0:T(8,128)S(1)} %fusion.204), channel_id=6, replica_groups=mesh['horizon_0'=8,'horizon_1'=4,'batch'=8] {'horizon_0'}, dimensions={0}, use_global_device_ids=true | all-gather | bytes 82944 | tf_op jit(solution)/shard_map/all_gather | solution.py:102
  205.1 8.0 %all-gather.9 = f32[4,1,48]{2,1,0:T(1,128)S(1)} all-gather(f32[1,1,48]{2,1,0:T(1,128)} %bitcast.748), channel_id=7, replica_groups=mesh['horizon_0'=8,'horizon_1'=4,'batch'=8] {'horizon_1'}, dimensions={0}, use_global_device_ids=true | all-gather | bytes 960 | tf_op jit(solution)/shard_map/all_gather | solution.py:102
  215.8 1.5 fusion.96
  217.9 1.4 dynamic-update-slice
  219.2 17.0 %all-reduce = f32[384]{0:T(512)S(1)} all-reduce(f32[384]{0:T(512)} %dynamic-update-slice), channel_id=8, replica_groups=mesh['horizon_0'=8,'horizon_1'=4,'batch'=8] {'horizon_0'}, use_global_device_ids=true, to_apply=%add | all-reduce | flops 384 | bytes 3072
  239.0 1.6 fusion.106
  240.6 10.9 %all-gather.15.cloned.1.call-done = f32[384,4096]{1,0:T(8,128)} async-done(((f32[48,4096]{1,0:T(8,128)}), f32[384,4096]{1,0:T(8,128)}) %all-gather.15.cloned.1.call-update) | async-done | bytes 6291472 | tf_op jit(solution)/shard_map/all_gather | solution.py:102
  251.5 1.8 convolution_add_fusion.8
  253.3 2.2 convolution_add_fusion.7
  255.5 2.0 convolution_add_fusion.6
  260.9 1.0 fusion.82
  263.0 21.2 %while.99 = (s32[]{:T(128)}, f32[1,48,4096]{2,1,0:T(8,128)S(1)}, f32[1,48]{1,0:T(1,128)S(1)}, f32[8,1,16,4096]{3,2,1,0:T(8,128)S(1)}, f32[8,1,16]{2,1,0:T(1,128)...) while((s32[]{:T(128)}, f32[1,48,4096]{2,1,0:T(8,128)S(1)}, ...), condition=%wide.region_11.12_spmd, body=%wide.region_10.11_spmd.sunk | while | flops 152211552 | bytes 4831449 | solution.py:238
  284.2 3.7 %copy.68 = f32[1,128,4096]{1,0,2:T(1,128)} copy(f32[1,128,4096]{2,1,0:T(8,128)S(1)} %bitcast.721) | data formatting | bytes 4194304 | tf_op jit(solution)/shard_map/reshape;transpose | solution.py:244
  287.9 7.3 %all-to-all-start.1 = ((f32[1,128,4096]{1,0,2:T(1,128)}), f32[1,128,4096]{1,0,2:T(1,128)}, u32[]{:S(2)}, u32[]{:S(2)}) async-start(f32[1,128,4096]{1,0,2:T(1,128)} %copy.68), calls=%async_computation.1 | async-start | bytes 4194304 | tf_op jit(solution)/shard_map/all_to_all | solution.py:246
  297.7 47.6 %all-to-all-done.1 = f32[1,128,4096]{1,0,2:T(1,128)} async-done(((f32[1,128,4096]{1,0,2:T(1,128)}), f32[1,128,4096]{1,0,2:T(1,128)}, u32[]{:S(2)}, u32[]{:S(2)}) %all-to-all-start.1) | async-done | bytes 2097184 | tf_op jit(solution)/shard_map/all_to_all | solution.py:246
  345.3 4.1 %copy.98 = f32[1,128,32,128]{1,2,3,0:T(8,128)} copy(f32[1,128,32,128]{1,3,2,0:T(8,128)} %bitcast.183) | data formatting | bytes 4194304 | tf_op jit(solution)/shard_map/reshape | solution.py:248
  349.4 2.8 reshape.1040
  352.2 1.9 add.411
  354.2 1.3 copy-done.7
  (412 shorter events, 84.4 us)
Async XLA Ops:
  7.2 87.4 %copy-start = (f32[1,48]{1,0:T(1,128)S(1)}, f32[1,48]{1,0:T(1,128)}, u32[]{:S(2)}) copy-start(f32[1,48]{1,0:T(1,128)} %param.25) | copy-start | bytes 580
  7.2 28.0 %copy-start.9 = (f32[1,8,48,48]{3,2,1,0:T(8,128)S(1)}, f32[1,8,48,48]{3,2,1,0:T(8,128)}, u32[]{:S(2)}) copy-start(f32[1,8,48,48]{3,2,1,0:T(8,128)} %param.21) | copy-start | bytes 221188
  21.9 13.3 %copy-start.1 = (f32[8,1,48,48]{3,2,1,0:T(8,128)S(1)}, f32[8,1,48,48]{3,2,1,0:T(8,128)}, u32[]{:S(2)}) copy-start(f32[8,1,48,48]{3,2,1,0:T(8,128)} %get-tuple-element.1208) | copy-start | bytes 221188
  23.8 63.9 %all-to-all-start = ((f32[32,1,2352]{2,1,0:T(1,128)}), f32[32,1,2352]{2,1,0:T(1,128)S(1)}, u32[]{:S(2)}, u32[]{:S(2)}) async-start(f32[32,1,2352]{2,1,0:T(1,128)} %reshape.1195), calls=%async_computation | async-start | bytes 622592 | tf_op jit(solution)/shard_map/all_to_all | solution.py:17
  35.1 133.9 %all-gather.13.cloned.1.call-start = ((), (), s32[]{:S(2)}) async-start(), calls=%async_computation.2 | async-start | bytes 3932160 | tf_op jit(solution)/shard_map/all_gather | solution.py:102
  79.7 7.6 %copy-start.10 = (f32[1,8,48,16]{2,3,1,0:T(8,128)S(1)}, f32[1,8,48,16]{2,3,1,0:T(8,128)}, u32[]{:S(2)}) copy-start(f32[1,8,48,16]{2,3,1,0:T(8,128)} %param.20) | copy-start | bytes 73732
  125.7 0.7 copy-start.12
  126.4 44.4 %copy-start.13 = (f32[8,1,48,16]{2,3,0,1:T(8,128)}, f32[8,1,48,16]{2,3,0,1:T(8,128)S(1)}, u32[]{:S(2)}) copy-start(f32[8,1,48,16]{2,3,0,1:T(8,128)S(1)} %get-tuple-element.1225) | copy-start | bytes 73732
  126.4 46.4 %copy-start.20 = (f32[1,48]{1,0:T(1,128)}, f32[1,48]{1,0:T(1,128)S(1)}, u32[]{:S(2)}) copy-start(f32[1,48]{1,0:T(1,128)S(1)} %get-tuple-element.664) | copy-start | bytes 580
  126.5 0.9 copy-start.5
  127.4 124.2 %all-gather.15.cloned.1.call-start = ((), (), s32[]{:S(2)}) async-start(), calls=%async_computation.3 | async-start | bytes 7077888 | tf_op jit(solution)/shard_map/all_gather | solution.py:102
  139.5 37.6 %copy-start.8 = (f32[4,48,48]{2,1,0:T(8,128)}, f32[4,48,48]{2,1,0:T(8,128)S(1)}, u32[]{:S(2)}) copy-start(f32[4,48,48]{2,1,0:T(8,128)S(1)} %all-gather.2) | copy-start | bytes 110596
  169.0 3.8 %copy-start.6 = (f32[4,1,48,4096]{3,2,1,0:T(8,128)S(1)}, f32[4,1,48,4096]{3,2,1,0:T(8,128)}, u32[]{:S(2)}) copy-start(f32[4,1,48,4096]{3,2,1,0:T(8,128)} %all-gather.13.cloned.1.call-done) | copy-start | bytes 9437188
  173.6 1.8 copy-start.21
  175.4 63.6 %copy-start.2 = (f32[48,4096]{1,0:T(8,128)S(1)}, f32[48,4096]{1,0:T(8,128)}, u32[]{:S(2)}) copy-start(f32[48,4096]{1,0:T(8,128)} %convolution_add_fusion.9) | copy-start | bytes 2359300
  214.0 3.2 copy-start.17
  214.9 2.4 copy-start.18
  215.8 1.5 copy-start.19
  251.5 6.0 %copy-start.3 = (f32[384,4096]{1,0:T(8,128)S(1)}, f32[384,4096]{1,0:T(8,128)}, u32[]{:S(2)}) copy-start(f32[384,4096]{1,0:T(8,128)} %all-gather.15.cloned.1.call-done) | copy-start | bytes 18874372
  260.8 1.1 copy-start.4
  260.8 1.1 copy-start.15
  262.0 1.1 copy-start.11
  287.9 7.3 %copy-start.16 = (f32[1,8,16,16]{3,2,1,0:T(8,128)S(1)}, f32[1,8,16,16]{3,2,1,0:T(8,128)}, u32[]{:S(2)}) copy-start(f32[1,8,16,16]{3,2,1,0:T(8,128)} %param.22) | copy-start | bytes 24580
  287.9 7.4 %copy-start.14 = (f32[8,1,48,16]{2,3,0,1:T(8,128)S(1)}, f32[8,1,48,16]{2,3,0,1:T(8,128)}, u32[]{:S(2)}) copy-start(f32[8,1,48,16]{2,3,0,1:T(8,128)} %copy-done.13) | copy-start | bytes 73732
  287.9 57.4 %all-to-all-start.1 = ((f32[1,128,4096]{1,0,2:T(1,128)}), f32[1,128,4096]{1,0,2:T(1,128)}, u32[]{:S(2)}, u32[]{:S(2)}) async-start(f32[1,128,4096]{1,0,2:T(1,128)} %copy.68), calls=%async_computation.1 | async-start | bytes 4194304 | tf_op jit(solution)/shard_map/all_to_all | solution.py:246
  354.1 1.3 copy-start.7
Sparse Core Ops, SparseCore 0:
  127.5 41.4 all-gather.12
  175.5 75.9 all-gather.14
where the time goes:
time: 365 us; the launch traced here: 362 us
  blocking collectives  102 us (28%)
  matrix products  93 us (25%)
  waiting for transfers between devices  88 us (24%)
  local copies, waits for them, and re-layouts  32.8 us (9%)
  starting transfers between devices  18.7 us (5%)
  between operations  15.7 us (4%)
  loops' own time  7.11 us (2%)
  other arithmetic  4.63 us (1%)
    all_to_all x1, waiting for transfers between devices, body(): lax.all_to_all(upper, HORIZON, split_axis=2, concat_axis=2, tiled=True)  47.6 us
    all_gather x3, blocking collectives, prefix_by_axis(): pieces = jax.tree.map(lambda part: lax.all_gather(part, axis), subtotal)  47.2 us
    dot_general x76, matrix products, trans_mat(): return jnp.einsum('pji,pjk->pik', left, right, precision=HI)  44.6 us
    all_gather x2, waiting for transfers between devices, prefix_by_axis(): pieces = jax.tree.map(lambda part: lax.all_gather(part, axis), subtotal)  40.4 us
    all_gather x2, blocking collectives, collected_together(): both, at, found = (lax.all_gather(jnp.concatenate(lines), axis), 0, {})  38.2 us
    dot_general x30, matrix products, times_vec(): return jnp.einsum('pij,pj->pi', left, vector, precision=HI)  22.1 us
    unnamed x1, blocking collectives  17 us
    dot_general x53, matrix products, times_mat(): return jnp.einsum('pij,pjk->pik', left, right, precision=HI)  15.4 us
  transfers between devices with their start and end apart: 4, of which 3 were waited for; matrix products, arithmetic and copies ran while one was open for 8% of the time, Pallas kernels for 0%

commit v1 on v0

v1 whole, which is shorter than its diff:
```python
import functools

import jax
import jax.numpy as jnp
from jax import lax
from jax.experimental import pallas as pl
from jax.experimental.pallas import tpu as pltpu
from jax.sharding import PartitionSpec as P

NX = 48
NU = 16
SEC = 8
COLS = SEC * NU
GX = 4
GZ = 8
F32 = jnp.float32
BF16 = jnp.bfloat16
Z_ORDER = (4, 3, 5, 2, 6, 1, 7)
ARRIVE = (1, 7, 2, 6, 3, 5, 4)


def split(a):
    high = a.astype(BF16)
    return high, (a - high.astype(F32)).astype(BF16)


def dot(a, b):
    return lax.dot_general(a, b, (((1,), (0,)), ((), ())), preferred_element_type=F32)


def mm(a, b):
    ah, al = split(a)
    bh, bl = split(b)
    return dot(ah, bh) + (dot(ah, bl) + dot(al, bh))


def sq(a):
    return a[:, :NX]


def transposed(a):
    return jnp.transpose(jnp.concatenate([a, jnp.zeros((128 - a.shape[0], 128), F32)], axis=0))


def body(
    a_hbm, b_hbm, q_hbm, r_hbm, d_hbm, t_hbm, i_hbm,
    h_ref, grad_ref,
    a_v, b_v, q_v, r_v, d_v, t_v, i_v,
    y_v, qy_v, x_tc, x_lr, z_tc, z_l, z_r, coef_a, coef_b, rhs,
    in_sem, xt_s, xt_r, xl_s, xl_r, zt_s, zt_r, zl_s, zl_r, zr_s, zr_r, w_s, w_r,
):
    me = lax.axis_index("horizon")
    z, x = me // GX, me % GX

    loads = [
        pltpu.make_async_copy(src.at[0], dst, in_sem.at[k])
        for k, (src, dst) in enumerate(
            ((a_hbm, a_v), (b_hbm, b_v), (d_hbm, d_v), (t_hbm, t_v), (q_hbm, q_v), (r_hbm, r_v))
        )
    ]
    loads.append(pltpu.make_async_copy(i_hbm, i_v, in_sem.at[6]))
    for load in loads:
        load.start()

    for g in range(GZ):
        z_r[g] = jnp.zeros((NX, COLS), F32)

    def x_peer(d):
        return z * GX + (x + d) % GX

    def z_peer(d):
        return ((z + d) % GZ) * GX + x

    barrier = pltpu.get_barrier_semaphore()
    for d in range(1, GX):
        pl.semaphore_signal(barrier, inc=1, device_id={"horizon": x_peer(d)}, device_id_type=pl.DeviceIdType.MESH)
    for d in range(1, GZ):
        pl.semaphore_signal(barrier, inc=1, device_id={"horizon": z_peer(d)}, device_id_type=pl.DeviceIdType.MESH)

    def remote(ref, send, recv, peer):
        return pltpu.make_async_remote_copy(
            src_ref=ref, dst_ref=ref, send_sem=send, recv_sem=recv,
            device_id={"horizon": peer}, device_id_type=pl.DeviceIdType.MESH,
        )

    for load in loads:
        load.wait()

    lane = lax.broadcasted_iota(jnp.int32, (NX, 128), 1)
    row = lax.broadcasted_iota(jnp.int32, (NX, 128), 0)
    unit = jnp.where(lane == row, 1.0, 0.0).astype(F32)

    vectors = jnp.concatenate(
        [
            jnp.concatenate([d_v[...], t_v[...], jnp.broadcast_to(i_v[...], (8, NX))], axis=0),
            jnp.zeros((24, 128 - NX), F32),
        ],
        axis=1,
    )
    columns = transposed(vectors)[:NX]

    def vector_at(k):
        return jnp.where(lane == NX, pltpu.roll(columns, (NX - k) % 128, 1), 0.0)

    wide = jnp.zeros((NX, 128 - NX), F32)
    state = None
    for t in range(SEC):
        entry = vector_at(t)
        placed = jnp.concatenate([b_v[t], jnp.zeros((NX, 128 - NU), F32)], axis=1)
        if t:
            placed = pltpu.roll(placed, NU * t, 1)
        added = jnp.concatenate([entry, placed], axis=1)
        if t == 0:
            state = added + jnp.concatenate([a_v[0], wide, jnp.zeros((NX, 128), F32)], axis=1)
        else:
            state = mm(a_v[t], state) + added
        error = jnp.concatenate([state[:, :128] - vector_at(SEC + t), state[:, 128:]], axis=1)
        y_v[NX * t : NX * (t + 1), :] = error
        qy_v[NX * t : NX * (t + 1), :] = mm(q_v[t], error)
    gram = mm(jnp.transpose(y_v[...]), qy_v[...])
    own_l = state[:, 128:]
    own_r = gram[:NX, 128:]
    own_t = sq(state)
    x_tc[x] = state[:, :128] + pltpu.roll(gram[:NX, :128], 64, 1)
    x_lr[x, 0] = own_l
    x_lr[x, 1] = own_r

    pl.semaphore_wait(barrier, GX - 1 + GZ - 1)
    sends = []

    def send(ref, s, r, peer):
        copy = remote(ref, s, r, peer)
        copy.start()
        sends.append(copy)

    for d in (2, 1, 3):
        send(x_tc.at[x], xt_s.at[d], xt_r.at[x], x_peer(d))
    for d in (2, 1, 3):
        send(x_lr.at[x], xl_s.at[d], xl_r.at[x], x_peer(d))

    for d in range(1, GX):
        i = (x + d) % GX
        remote(x_tc.at[i], xt_s.at[d], xt_r.at[i], x_peer(d)).wait_recv()

    def unpack(packed):
        maps, costs = [], []
        for i in range(packed.shape[0]):
            both = packed[i]
            maps.append(jnp.where(lane < 64, both, 0.0))
            costs.append(jnp.where(lane < 64, pltpu.roll(both, 64, 1), 0.0))
        return maps, costs, [transposed(m)[:NX] for m in maps]

    def fold(tail, m, c, mt):
        inner = mm(sq(tail), m) + jnp.where(lane == NX, tail, 0.0)
        return c + mm(sq(mt), inner)

    def choose(index, values):
        out = values[0]
        for k in range(1, len(values)):
            out = jnp.where(index == k, values[k], out)
        return out

    nothing = jnp.zeros((NX, 128), F32)

    xm, xc, xmt = unpack(x_tc)
    tails = [None] * GX
    tail = nothing
    for i in reversed(range(GX)):
        tails[i] = tail
        tail = fold(tail, xm[i], xc[i], xmt[i])
    group_cost = tail
    before = [unit]
    for i in range(GX):
        if i == 0:
            before.append(xm[0])
        else:
            before.append(mm(sq(xm[i]), before[i]) + jnp.where(lane == NX, xm[i], 0.0))
    after = [None] * GX
    after[GX - 1] = unit
    after[GX - 2] = jnp.where(lane < NX, xm[GX - 1], 0.0)
    for i in reversed(range(GX - 2)):
        after[i] = mm(sq(after[i + 1]), jnp.where(lane < NX, xm[i + 1], 0.0))
    group_map = before[GX]
    own_mt = choose(x, xmt)
    own_before = choose(x, before[:GX])
    own_before_t = transposed(jnp.where(lane < NX, own_before, 0.0))[:NX]
    group_l = mm(sq(choose(x, after)), own_l)
    group_r = mm(
        sq(own_before_t), own_r + mm(sq(own_mt), mm(sq(choose(x, tails)), own_l))
    )
    z_tc[z] = group_map + pltpu.roll(group_cost, 64, 1)
    z_l[z] = group_l
    z_r[z] = group_r

    for d in Z_ORDER:
        send(z_tc.at[z], zt_s.at[d], zt_r.at[z], z_peer(d))
    for d in Z_ORDER:
        send(z_l.at[z], zl_s.at[d], zl_r.at[z], z_peer(d))
    for d in Z_ORDER:
        @pl.when((z + d) % GZ < z)
        def _():
            remote(z_r.at[z], zr_s.at[d], zr_r.at[z], z_peer(d)).start()

    for d in range(1, GZ):
        g = (z + d) % GZ
        remote(z_tc.at[g], zt_s.at[d], zt_r.at[g], z_peer(d)).wait_recv()

    zm, zc, zmt = unpack(z_tc)
    tail = nothing
    z_tails = [None] * GZ
    for g in reversed(range(GZ)):
        z_tails[g] = tail
        if g:
            tail = fold(tail, zm[g], zc[g], zmt[g])
    carry = unit
    backs = []
    for g in range(GZ):
        nxt = carry if g == 0 else jnp.where(g > z + 1, mm(sq(carry), zmt[g - 1]), unit)
        backs.append(jnp.where(lane < NX, nxt, 0.0))
        carry = backs[g]
    backs.append(jnp.where(lane < NX, mm(sq(carry), zmt[GZ - 1]), 0.0))
    carry = unit
    fronts = [None] * GZ
    for g in reversed(range(GZ)):
        fronts[g] = carry if g == GZ - 1 else jnp.where(g < z - 1, mm(sq(carry), zm[g + 1]), unit)
        carry = jnp.where(lane < NX, fronts[g], 0.0)
        fronts[g] = carry
    for g in range(GZ):
        coef_a[g] = jnp.where(g > z, backs[g], nothing)
        coef_b[g] = jnp.where(g > z, mm(sq(backs[g + 1]), z_tails[g]), fronts[g])
    enter = vector_at(2 * SEC)
    for g in range(GZ - 1):
        enter = jnp.where(g < z, mm(sq(zm[g]), enter) + jnp.where(lane == NX, zm[g], 0.0), enter)
    group_tail = choose(z, z_tails)

    for d in ARRIVE:
        g = (z + d) % GZ
        remote(z_l.at[g], zl_s.at[d], zl_r.at[g], z_peer(d)).wait_recv()

        @pl.when(g > z)
        def _():
            remote(z_r.at[g], zr_s.at[d], zr_r.at[g], z_peer(d)).wait_recv()

        rhs[g, x] = mm(sq(coef_a[g]), z_r[g]) + mm(sq(coef_b[g]), z_l[g])
        for e in range(1, GX):
            send(rhs.at[g, x], w_s.at[d, e], w_r.at[g, x], x_peer(e))

    for d in range(1, GX):
        i = (x + d) % GX
        remote(x_lr.at[i], xl_s.at[d], xl_r.at[i], x_peer(d)).wait_recv()
    tail = group_tail
    for i in reversed(range(GX)):
        tails[i] = tail
        if i:
            tail = fold(tail, xm[i], xc[i], xmt[i])
    own_tail = choose(x, tails)
    carry = unit
    backs = []
    for i in range(GX):
        nxt = carry if i == 0 else jnp.where(i > x + 1, mm(sq(carry), xmt[i - 1]), unit)
        backs.append(jnp.where(lane < NX, nxt, 0.0))
        carry = backs[i]
    backs.append(jnp.where(lane < NX, mm(sq(carry), xmt[GX - 1]), 0.0))
    carry = unit
    for i in reversed(range(GX)):
        front = carry if i == GX - 1 else jnp.where(i < x - 1, mm(sq(carry), xm[i + 1]), unit)
        carry = jnp.where(lane < NX, front, 0.0)
        ca = jnp.where(i > x, backs[i], nothing)
        cb = jnp.where(i > x, mm(sq(backs[i + 1]), tails[i]), jnp.where(i == x, own_tail, carry))
        rhs[z, i] = mm(sq(ca), x_lr[i, 1]) + mm(sq(cb), x_lr[i, 0])

    entering = mm(sq(own_before), enter) + jnp.where((lane == NX) & (x > 0), own_before, 0.0)
    leaving = mm(own_t, entering) + jnp.where(lane == NX, state[:, :128], 0.0)
    costate = mm(sq(own_tail), leaving) + jnp.where(lane == NX, own_tail, 0.0)
    grad_ref[...] = gram[NX : NX + 1, 128:] + jnp.sum(
        entering[:, NX : NX + 1] * own_r + costate[:, NX : NX + 1] * own_l, axis=0, keepdims=True
    )

    full_r = own_r + mm(sq(own_mt), mm(sq(own_tail), own_l))
    group_mt = transposed(jnp.where(lane < NX, group_map, 0.0))[:NX]
    group_full = group_r + mm(sq(group_mt), mm(sq(group_tail), group_l))

    def factors(value):
        high, low = split(value)
        turned = jnp.transpose(
            jnp.concatenate([high.astype(F32), low.astype(F32), jnp.zeros((32, 128), F32)], axis=0)
        )
        return turned.astype(BF16)[:, : 2 * NX]

    def rows(left, right):
        high, low = split(right)
        return dot(left, jnp.concatenate([high, high], axis=0)) + dot(left[:, :NX], low)

    f_gl, f_gr = factors(group_l), factors(group_full)
    f_l, f_r = factors(own_l), factors(full_r)

    tile = gram[128:, 128:]
    cost = jnp.concatenate(
        [
            jnp.concatenate([r_v[t], jnp.zeros((NU, 128 - NU), F32)], axis=1)
            if t == 0
            else pltpu.roll(jnp.concatenate([r_v[t], jnp.zeros((NU, 128 - NU), F32)], axis=1), NU * t, 1)
            for t in range(SEC)
        ],
        axis=0,
    )
    for i in range(GX):
        left = jnp.where(i < x, f_r.astype(F32), f_l.astype(F32)).astype(BF16)
        block = rows(left, rhs[z, i])
        block = block + jnp.where(i == x, tile + cost, 0.0)
        h_ref[:, pl.ds(pl.multiple_of(z * (GX * COLS) + i * COLS, COLS), COLS)] = block

    for d in ARRIVE:
        g = (z + d) % GZ
        left = jnp.where(g > z, f_gl.astype(F32), f_gr.astype(F32)).astype(BF16)
        for e in range(1, GX):
            i = (x + e) % GX
            remote(rhs.at[g, i], w_s.at[d, e], w_r.at[g, i], x_peer(e)).wait_recv()
        right = jnp.concatenate([rhs[g, i] for i in range(GX)], axis=1)
        h_ref[:, pl.ds(pl.multiple_of(g * (GX * COLS), GX * COLS), GX * COLS)] = rows(left, right)

    for copy in sends:
        copy.wait_send()
    for d in Z_ORDER:
        @pl.when((z + d) % GZ < z)
        def _():
            remote(z_r.at[z], zr_s.at[d], zr_r.at[z], z_peer(d)).wait_send()


def condense(dynamics, inputs, state_cost, input_cost, drift, target, initial):
    dma = pltpu.SemaphoreType.DMA
    hessian, gradient = pl.pallas_call(
        body,
        out_shape=(
            jax.ShapeDtypeStruct((COLS, GX * GZ * COLS), F32),
            jax.ShapeDtypeStruct((1, COLS), F32),
        ),
        in_specs=[pl.BlockSpec(memory_space=pl.ANY)] * 7,
        out_specs=(
            pl.BlockSpec(memory_space=pltpu.VMEM),
            pl.BlockSpec(memory_space=pltpu.VMEM),
        ),
        scratch_shapes=[
            pltpu.VMEM((SEC, NX, NX), F32),
            pltpu.VMEM((SEC, NX, NU), F32),
            pltpu.VMEM((SEC, NX, NX), F32),
            pltpu.VMEM((SEC, NU, NU), F32),
            pltpu.VMEM((SEC, NX), F32),
            pltpu.VMEM((SEC, NX), F32),
            pltpu.VMEM((1, NX), F32),
            pltpu.VMEM((SEC * NX, 256), F32),
            pltpu.VMEM((SEC * NX, 256), F32),
            pltpu.VMEM((GX, NX, 128), F32),
            pltpu.VMEM((GX, 2, NX, COLS), F32),
            pltpu.VMEM((GZ, NX, 128), F32),
            pltpu.VMEM((GZ, NX, COLS), F32),
            pltpu.VMEM((GZ, NX, COLS), F32),
            pltpu.VMEM((GZ, NX, 128), F32),
            pltpu.VMEM((GZ, NX, 128), F32),
            pltpu.VMEM((GZ, GX, NX, COLS), F32),
            dma((7,)),
            dma((GX,)), dma((GX,)), dma((GX,)), dma((GX,)),
            dma((GZ,)), dma((GZ,)), dma((GZ,)), dma((GZ,)), dma((GZ,)), dma((GZ,)),
            dma((GZ, GX)), dma((GZ, GX)),
        ],
        compiler_params=pltpu.CompilerParams(collective_id=0, has_side_effects=True),
        name="condense",
    )(dynamics, inputs, state_cost, input_cost, drift, target, initial)
    return hessian[None], gradient


def solution(mesh):
    return jax.shard_map(
        condense,
        mesh=mesh,
        in_specs=(
            P("batch", "horizon", None, None),
            P("batch", "horizon", None, None),
            P("batch", "horizon", None, None),
            P("batch", "horizon", None, None),
            P("batch", "horizon", None),
            P("batch", "horizon", None),
            P("batch", None),
        ),
        out_specs=(P("batch", "horizon", None), P("batch", "horizon")),
        check_vma=False,
    )
```

time: 365 us -> 46.1 us (0.13)
  blocking collectives: 102 us -> 0 us
  matrix products: 93 us -> 0 us
  waiting for transfers between devices: 88 us -> 0 us
  Pallas kernels: 0 us -> 40 us
  local copies, waits for them, and re-layouts: 32.8 us -> 5.26 us
  starting transfers between devices: 18.7 us -> 0 us
  between operations: 15.7 us -> 0.65 us
  loops' own time: 7.11 us -> 0 us
  other arithmetic: 4.63 us -> 0 us
    dot_general x199 -> x0, matrix products: 93 us -> none  [the longest x76 44.6 us: trans_mat(): return jnp.einsum('pji,pjk->pik', left, right, precision=HI)]
    all_gather x5 -> x0, blocking collectives: 85.4 us -> none  [the longest x3 47.2 us: prefix_by_axis(): pieces = jax.tree.map(lambda part: lax.all_gather(part, axis), subtotal)]
    all_to_all x2 -> x0, waiting for transfers between devices: 47.6 us -> none  [the longest x1 47.6 us: body(): lax.all_to_all(upper, HORIZON, split_axis=2, concat_axis=2, tiled=True)]
    all_gather x2 -> x0, waiting for transfers between devices: 40.4 us -> none  [prefix_by_axis(): pieces = jax.tree.map(lambda part: lax.all_gather(part, axis), subtotal)]
    pallas_call x0 -> x1, Pallas kernels: none -> 40 us  [condense(): pl.pallas_call(body, out_shape=(jax.ShapeDtypeStruct((COLS, GX * GZ * COL...]
    all_to_all x2 -> x0, starting transfers between devices: 18.6 us -> none  [the longest x1 11.3 us: copy_for_each(): return lax.all_to_all(copies, axis, split_axis=0, concat_axis=0, tiled=True)]
    unnamed x1 -> x0, blocking collectives: 17 us -> none
    another operation x6 -> x0, loops' own time: 7.11 us -> none  [the longest x1 5.73 us: body(): lax.scan(sweep_compact, compact_start, (section_dynamics, value_cols, wei...]
  transfers between devices with their start and end apart: 4 -> 0, of which waited for: 3 -> 0; matrix products, arithmetic and copies ran while one was open for 8% -> 0% of each run, Pallas kernels for 0% -> 0%
where the time goes in v1:
time: 46.1 us; the launch traced here: 45.9 us
  Pallas kernels  40 us (87%)
  local copies, waits for them, and re-layouts  5.26 us (11%)
  between operations  0.65 us (1%)
    pallas_call x1, Pallas kernels, condense(): pl.pallas_call(body, out_shape=(jax.ShapeDtypeStruct((COLS, GX * GZ * COL...  40 us
    unnamed x5, local copies, waits for them, and re-layouts  5.26 us

profile of v1, /device:TPU:8, one launch (start us, length us, event | category | flops | bytes accessed | tf_op | source)
XLA Modules:
  0.0 45.9 jit_solution(5335955584872628206)
XLA Ops:
  0.6 1.6 %copy.9.b_hbm = f32[1,8,48,16]{3,2,1,0:T(8,128)} copy(f32[1,8,48,16]{2,3,1,0:T(8,128)} %param.8) | data formatting | bytes 49152 | tf_op args[1]
  2.3 40.0 %condense.1 = (f32[128,4096]{1,0:T(8,128)}, f32[1,128]{1,0:T(1,128)}) custom-call(f32[1,8,48,48]{3,2,1,0:T(8,128)} %a_hbm.1, f32[1,8,48,16]{3,2,1,0:T(8,128)} %copy.9.b_hbm, f32[1,8,48,48]{3,2,1,0:T(8,128)} %q_hbm.1, f32[1,8,16,16]{3,2,1,0:T(8,128)} %r_hbm.1, f32[1,8,48]{2,1,0:T(8,128)} %d_hbm.1, f32[1,8,48]{2,1,0:T(8,128)} %t_hbm.1, f32[1,48]{1,0:T(1,128)} %i_hbm.1), custom_call_target="tpu_custom_call" | custom-call | tf_op jit(solution)/shard_map/condense/pallas_call | solution.py:332
  42.3 0.0 copy-start
  42.3 3.1 %copy.12 = f32[1,128,4096]{2,1,0:T(8,128)} copy(f32[1,128,4096]{2,1,0:T(8,128)} %bitcast.1) | data formatting | bytes 4194304
  45.4 0.0 copy-done
  45.4 0.5 %copy.13 = f32[1,128]{1,0:T(1,128)} copy(f32[1,128]{1,0:T(1,128)S(1)} %copy-done) | data formatting | bytes 1024
Async XLA Ops:
  42.3 3.1 %copy-start = (f32[1,128]{1,0:T(1,128)S(1)}, f32[1,128]{1,0:T(1,128)}, u32[]{:S(2)}) copy-start(f32[1,128]{1,0:T(1,128)} %get-tuple-element.9) | copy-start | bytes 1540

commit v2 on v1

--- a/solution.py
+++ b/solution.py
@@ -17,6 +17,7 @@
 BF16 = jnp.bfloat16
 Z_ORDER = (4, 3, 5, 2, 6, 1, 7)
 ARRIVE = (1, 7, 2, 6, 3, 5, 4)
+RELAYED = 0
 
 
 def split(a):
@@ -98,17 +99,19 @@
         axis=1,
     )
     columns = transposed(vectors)[:NX]
+    init_row = vectors[2 * SEC : 2 * SEC + 1]
 
     def vector_at(k):
         return jnp.where(lane == NX, pltpu.roll(columns, (NX - k) % 128, 1), 0.0)
 
     wide = jnp.zeros((NX, 128 - NX), F32)
+    controls = jnp.transpose(
+        jnp.concatenate([b_v[...].reshape(COLS, NX), jnp.zeros((COLS, 128 - NX), F32)], axis=1)
+    )[:NX]
     state = None
     for t in range(SEC):
         entry = vector_at(t)
-        placed = jnp.concatenate([b_v[t], jnp.zeros((NX, 128 - NU), F32)], axis=1)
-        if t:
-            placed = pltpu.roll(placed, NU * t, 1)
+        placed = jnp.where(lane // NU == t, controls, 0.0)
         added = jnp.concatenate([entry, placed], axis=1)
         if t == 0:
             state = added + jnp.concatenate([a_v[0], wide, jnp.zeros((NX, 128), F32)], axis=1)
@@ -142,17 +145,20 @@
         i = (x + d) % GX
         remote(x_tc.at[i], xt_s.at[d], xt_r.at[i], x_peer(d)).wait_recv()
 
-    def unpack(packed):
-        maps, costs = [], []
-        for i in range(packed.shape[0]):
-            both = packed[i]
-            maps.append(jnp.where(lane < 64, both, 0.0))
-            costs.append(jnp.where(lane < 64, pltpu.roll(both, 64, 1), 0.0))
-        return maps, costs, [transposed(m)[:NX] for m in maps]
-
-    def fold(tail, m, c, mt):
-        inner = mm(sq(tail), m) + jnp.where(lane == NX, tail, 0.0)
-        return c + mm(sq(mt), inner)
+    def turned(packed):
+        return transposed(packed)
+
+    def mixed(packed, flip):
+        return jnp.where(lane < NX, flip[:NX], jnp.where(lane < 64, 0.0, packed))
+
+    def maps_of(packed):
+        return jnp.where(lane < 64, packed, 0.0)
+
+    def cost_of(packed):
+        return jnp.where(lane < 64, pltpu.roll(packed, 64, 1), 0.0)
+
+    def at_column(value):
+        return jnp.where(lane == NX, value, 0.0)
 
     def choose(index, values):
         out = values[0]
@@ -162,41 +168,37 @@
 
     nothing = jnp.zeros((NX, 128), F32)
 
-    xm, xc, xmt = unpack(x_tc)
+    xp = [x_tc[i] for i in range(GX)]
+    xf = [turned(p) for p in xp]
+    xm = [maps_of(p) for p in xp]
+    backs = [unit, jnp.where(lane < NX, xf[0][:NX], 0.0)]
+    gains = [cost_of(xp[0])]
+    for i in range(1, GX):
+        both = mm(sq(backs[i]), mixed(xp[i], xf[i]))
+        backs.append(both)
+        gains.append(cost_of(both))
     tails = [None] * GX
-    tail = nothing
-    for i in reversed(range(GX)):
-        tails[i] = tail
-        tail = fold(tail, xm[i], xc[i], xmt[i])
-    group_cost = tail
-    before = [unit]
-    for i in range(GX):
-        if i == 0:
-            before.append(xm[0])
-        else:
-            before.append(mm(sq(xm[i]), before[i]) + jnp.where(lane == NX, xm[i], 0.0))
     after = [None] * GX
-    after[GX - 1] = unit
-    after[GX - 2] = jnp.where(lane < NX, xm[GX - 1], 0.0)
-    for i in reversed(range(GX - 2)):
-        after[i] = mm(sq(after[i + 1]), jnp.where(lane < NX, xm[i + 1], 0.0))
-    group_map = before[GX]
-    own_mt = choose(x, xmt)
-    own_before = choose(x, before[:GX])
-    own_before_t = transposed(jnp.where(lane < NX, own_before, 0.0))[:NX]
+    tails[GX - 1], after[GX - 1] = nothing, unit
+    tails[GX - 2], after[GX - 2] = gains[GX - 1], xm[GX - 1]
+    for i in reversed(range(GX - 1)):
+        stack = mm(sq(jnp.concatenate([tails[i], after[i]], axis=0)), xm[i])
+        low = stack[:NX] + at_column(tails[i]) + gains[i]
+        high = stack[NX:] + at_column(after[i])
+        if i:
+            tails[i - 1], after[i - 1] = low, high
+    group_cost, group_map = low, high
+    z_tc[z] = group_map + pltpu.roll(group_cost, 64, 1)
+    for d in Z_ORDER:
+        send(z_tc.at[z], zt_s.at[d], zt_r.at[z], z_peer(d))
+
     group_l = mm(sq(choose(x, after)), own_l)
-    group_r = mm(
-        sq(own_before_t), own_r + mm(sq(own_mt), mm(sq(choose(x, tails)), own_l))
-    )
-    z_tc[z] = group_map + pltpu.roll(group_cost, 64, 1)
+    group_r = mm(sq(choose(x, backs[:GX])), own_r) + mm(sq(choose(x, tails)), own_l)
     z_l[z] = group_l
     z_r[z] = group_r
-
-    for d in Z_ORDER:
-        send(z_tc.at[z], zt_s.at[d], zt_r.at[z], z_peer(d))
-    for d in Z_ORDER:
+    for d in ARRIVE:
         send(z_l.at[z], zl_s.at[d], zl_r.at[z], z_peer(d))
-    for d in Z_ORDER:
+    for d in ARRIVE:
         @pl.when((z + d) % GZ < z)
         def _():
             remote(z_r.at[z], zr_s.at[d], zr_r.at[z], z_peer(d)).start()
@@ -205,35 +207,38 @@
         g = (z + d) % GZ
         remote(z_tc.at[g], zt_s.at[d], zt_r.at[g], z_peer(d)).wait_recv()
 
-    zm, zc, zmt = unpack(z_tc)
-    tail = nothing
-    z_tails = [None] * GZ
-    for g in reversed(range(GZ)):
-        z_tails[g] = tail
-        if g:
-            tail = fold(tail, zm[g], zc[g], zmt[g])
-    carry = unit
-    backs = []
+    zp = [z_tc[g] for g in range(GZ)]
+    zf = [turned(p) for p in zp]
+    zm = [maps_of(p) for p in zp]
+    ups = [jnp.where(lane < NX, jnp.broadcast_to(init_row, (NX, 128)), 0.0)]
+    gains = []
     for g in range(GZ):
-        nxt = carry if g == 0 else jnp.where(g > z + 1, mm(sq(carry), zmt[g - 1]), unit)
-        backs.append(jnp.where(lane < NX, nxt, 0.0))
-        carry = backs[g]
-    backs.append(jnp.where(lane < NX, mm(sq(carry), zmt[GZ - 1]), 0.0))
-    carry = unit
-    fronts = [None] * GZ
-    for g in reversed(range(GZ)):
-        fronts[g] = carry if g == GZ - 1 else jnp.where(g < z - 1, mm(sq(carry), zm[g + 1]), unit)
-        carry = jnp.where(lane < NX, fronts[g], 0.0)
-        fronts[g] = carry
+        both = mm(sq(ups[g]), mixed(zp[g], zf[g]))
+        gains.append(jnp.where(g > z, cost_of(both), 0.0))
+        if g < GZ - 1:
+            moved = both + jnp.where(g < z, zf[g][NX : NX + 1], 0.0)
+            ups.append(jnp.where(lane < NX, jnp.where(g == z, unit, moved), 0.0))
+    enter = at_column(jnp.sum(jnp.where(lane == row, choose(z, ups), 0.0), axis=1, keepdims=True))
+    downs = [None] * GZ
+    downs[GZ - 1] = nothing
+    for g in reversed(range(1, GZ)):
+        if g == GZ - 1:
+            moved = gains[g]
+        else:
+            moved = mm(sq(downs[g]), zm[g]) + at_column(downs[g]) + gains[g]
+        downs[g - 1] = jnp.where(g == z, unit, moved)
     for g in range(GZ):
-        coef_a[g] = jnp.where(g > z, backs[g], nothing)
-        coef_b[g] = jnp.where(g > z, mm(sq(backs[g + 1]), z_tails[g]), fronts[g])
-    enter = vector_at(2 * SEC)
-    for g in range(GZ - 1):
-        enter = jnp.where(g < z, mm(sq(zm[g]), enter) + jnp.where(lane == NX, zm[g], 0.0), enter)
-    group_tail = choose(z, z_tails)
-
-    for d in ARRIVE:
+        coef_a[g] = jnp.where(g > z, ups[g], nothing)
+        coef_b[g] = downs[g]
+    group_tail = choose(z, downs)
+
+    def forward(k):
+        g = (z + ARRIVE[k]) % GZ
+        i = (x + 1) % GX
+        remote(rhs.at[g, i], w_s.at[ARRIVE[k], 1], w_r.at[g, i], x_peer(1)).wait_recv()
+        send(rhs.at[g, i], w_s.at[ARRIVE[k], 2], w_r.at[g, i], x_peer(3))
+
+    for k, d in enumerate(ARRIVE):
         g = (z + d) % GZ
         remote(z_l.at[g], zl_s.at[d], zl_r.at[g], z_peer(d)).wait_recv()
 
@@ -242,42 +247,43 @@
             remote(z_r.at[g], zr_s.at[d], zr_r.at[g], z_peer(d)).wait_recv()
 
         rhs[g, x] = mm(sq(coef_a[g]), z_r[g]) + mm(sq(coef_b[g]), z_l[g])
-        for e in range(1, GX):
+        if k >= RELAYED:
+            send(rhs.at[g, x], w_s.at[d, 2], w_r.at[g, x], x_peer(2))
+        for e in (3, 1):
             send(rhs.at[g, x], w_s.at[d, e], w_r.at[g, x], x_peer(e))
+        if 2 <= k < RELAYED + 2:
+            forward(k - 2)
 
     for d in range(1, GX):
         i = (x + d) % GX
         remote(x_lr.at[i], xl_s.at[d], xl_r.at[i], x_peer(d)).wait_recv()
-    tail = group_tail
-    for i in reversed(range(GX)):
-        tails[i] = tail
-        if i:
-            tail = fold(tail, xm[i], xc[i], xmt[i])
-    own_tail = choose(x, tails)
-    carry = unit
-    backs = []
+    ups = [unit]
+    gains = []
     for i in range(GX):
-        nxt = carry if i == 0 else jnp.where(i > x + 1, mm(sq(carry), xmt[i - 1]), unit)
-        backs.append(jnp.where(lane < NX, nxt, 0.0))
-        carry = backs[i]
-    backs.append(jnp.where(lane < NX, mm(sq(carry), xmt[GX - 1]), 0.0))
-    carry = unit
-    for i in reversed(range(GX)):
-        front = carry if i == GX - 1 else jnp.where(i < x - 1, mm(sq(carry), xm[i + 1]), unit)
-        carry = jnp.where(lane < NX, front, 0.0)
-        ca = jnp.where(i > x, backs[i], nothing)
-        cb = jnp.where(i > x, mm(sq(backs[i + 1]), tails[i]), jnp.where(i == x, own_tail, carry))
-        rhs[z, i] = mm(sq(ca), x_lr[i, 1]) + mm(sq(cb), x_lr[i, 0])
-
-    entering = mm(sq(own_before), enter) + jnp.where((lane == NX) & (x > 0), own_before, 0.0)
-    leaving = mm(own_t, entering) + jnp.where(lane == NX, state[:, :128], 0.0)
-    costate = mm(sq(own_tail), leaving) + jnp.where(lane == NX, own_tail, 0.0)
+        both = mm(sq(ups[i]), mixed(xp[i], xf[i]))
+        gains.append(jnp.where(i > x, cost_of(both), 0.0))
+        ups.append(jnp.where(lane < NX, jnp.where(i > x, both, unit), 0.0))
+    downs = [None] * GX
+    downs[GX - 1] = mm(sq(ups[GX]), group_tail)
+    for i in reversed(range(1, GX)):
+        moved = mm(sq(downs[i]), xm[i]) + at_column(downs[i]) + gains[i]
+        downs[i - 1] = jnp.where(i == x, unit, moved)
+    own_tail = choose(x, downs)
+    for i in range(GX):
+        ca = jnp.where(i > x, ups[i], nothing)
+        rhs[z, i] = mm(sq(ca), x_lr[i, 1]) + mm(sq(downs[i]), x_lr[i, 0])
+
+    for i in range(GX - 1):
+        enter = jnp.where(i < x, mm(sq(xm[i]), enter) + at_column(xm[i]), enter)
+    leaving = mm(own_t, enter) + at_column(state[:, :128])
+    costate = mm(sq(own_tail), leaving) + at_column(own_tail)
     grad_ref[...] = gram[NX : NX + 1, 128:] + jnp.sum(
-        entering[:, NX : NX + 1] * own_r + costate[:, NX : NX + 1] * own_l, axis=0, keepdims=True
+        enter[:, NX : NX + 1] * own_r + costate[:, NX : NX + 1] * own_l, axis=0, keepdims=True
     )
 
+    own_mt = choose(x, xf)[:NX]
     full_r = own_r + mm(sq(own_mt), mm(sq(own_tail), own_l))
-    group_mt = transposed(jnp.where(lane < NX, group_map, 0.0))[:NX]
+    group_mt = choose(z, zf)[:NX]
     group_full = group_r + mm(sq(group_mt), mm(sq(group_tail), group_l))
 
     def factors(value):
@@ -310,12 +316,13 @@
         block = block + jnp.where(i == x, tile + cost, 0.0)
         h_ref[:, pl.ds(pl.multiple_of(z * (GX * COLS) + i * COLS, COLS), COLS)] = block
 
-    for d in ARRIVE:
+    for k, d in enumerate(ARRIVE):
         g = (z + d) % GZ
         left = jnp.where(g > z, f_gl.astype(F32), f_gr.astype(F32)).astype(BF16)
         for e in range(1, GX):
             i = (x + e) % GX
-            remote(rhs.at[g, i], w_s.at[d, e], w_r.at[g, i], x_peer(e)).wait_recv()
+            if k >= RELAYED or e != 1:
+                remote(rhs.at[g, i], w_s.at[d, e], w_r.at[g, i], x_peer(e)).wait_recv()
         right = jnp.concatenate([rhs[g, i] for i in range(GX)], axis=1)
         h_ref[:, pl.ds(pl.multiple_of(g * (GX * COLS), GX * COLS), GX * COLS)] = rows(left, right)
 
@@ -335,14 +342,14 @@
             jax.ShapeDtypeStruct((COLS, GX * GZ * COLS), F32),
             jax.ShapeDtypeStruct((1, COLS), F32),
         ),
-        in_specs=[pl.BlockSpec(memory_space=pl.ANY)] * 7,
+        in_specs=[pl.BlockSpec(memory_space=pltpu.HBM)] * 7,
         out_specs=(
             pl.BlockSpec(memory_space=pltpu.VMEM),
             pl.BlockSpec(memory_space=pltpu.VMEM),
         ),
         scratch_shapes=[
             pltpu.VMEM((SEC, NX, NX), F32),
-            pltpu.VMEM((SEC, NX, NU), F32),
+            pltpu.VMEM((SEC, NU, NX), F32),
             pltpu.VMEM((SEC, NX, NX), F32),
             pltpu.VMEM((SEC, NU, NU), F32),
             pltpu.VMEM((SEC, NX), F32),
@@ -363,9 +370,11 @@
             dma((GZ,)), dma((GZ,)), dma((GZ,)), dma((GZ,)), dma((GZ,)), dma((GZ,)),
             dma((GZ, GX)), dma((GZ, GX)),
         ],
-        compiler_params=pltpu.CompilerParams(collective_id=0, has_side_effects=True),
+        compiler_params=pltpu.CompilerParams(
+            collective_id=0, has_side_effects=True, vmem_limit_bytes=16 * 1024 * 1024
+        ),
         name="condense",
-    )(dynamics, inputs, state_cost, input_cost, drift, target, initial)
+    )(*(pltpu.with_memory_space_constraint(v, pltpu.HBM) for v in (dynamics, jnp.swapaxes(inputs, 2, 3), state_cost, input_cost, drift, target, initial)))
     return hessian[None], gradient
 
 

time: 46.1 us -> 37.4 us (0.81)
  Pallas kernels: 40 us -> 34.8 us
  local copies, waits for them, and re-layouts: 5.26 us -> 1.83 us
    pallas_call x1, Pallas kernels: 40 us -> 34.8 us  [condense(): pl.pallas_call(body, out_shape=(jax.ShapeDtypeStruct((COLS, GX * GZ * COL...]
    unnamed x5 -> x2, local copies, waits for them, and re-layouts: 5.26 us -> 1.83 us
where the time goes in v2:
time: 37.4 us; the launch traced here: 37.3 us
  Pallas kernels  34.8 us (93%)
  local copies, waits for them, and re-layouts  1.83 us (5%)
  between operations  0.64 us (2%)
    pallas_call x1, Pallas kernels, condense(): pl.pallas_call(body, out_shape=(jax.ShapeDtypeStruct((COLS, GX * GZ * COL...  34.8 us
    unnamed x2, local copies, waits for them, and re-layouts  1.83 us

profile of v2, /device:TPU:8, one launch (start us, length us, event | category | flops | bytes accessed | tf_op | source)
XLA Modules:
  0.0 37.3 jit_solution(3255286523201203903)
XLA Ops:
  0.6 34.8 %condense.1 = (f32[128,4096]{1,0:T(8,128)S(1)}, f32[1,128]{1,0:T(1,128)S(1)}) custom-call(f32[1,8,48,48]{3,2,1,0:T(8,128)} %a_hbm.1, f32[1,8,16,48]{3,2,1,0:T(8,128)} %bitcast.3, f32[1,8,48,48]{3,2,1,0:T(8,128)} %q_hbm.1, f32[1,8,16,16]{3,2,1,0:T(8,128)} %r_hbm.1, f32[1,8,48]{2,1,0:T(8,128)} %d_hbm.1, f32[1,8,48]{2,1,0:T(8,128)} %t_hbm.1, f32[1,48]{1,0:T(1,128)} %i_hbm.1), custom_call_target="tpu_custom_call" | custom-call | tf_op jit(solution)/shard_map/condense/pallas_call | solution.py:339
  35.4 1.3 %copy.11 = f32[1,128,4096]{2,1,0:T(8,128)} copy(f32[1,128,4096]{2,1,0:T(8,128)S(1)} %bitcast.2) | data formatting | bytes 4194304
  36.8 0.5 %copy.12 = f32[1,128]{1,0:T(1,128)} copy(f32[1,128]{1,0:T(1,128)S(1)} %get-tuple-element.9) | data formatting | bytes 1024

commit v3 on v2

--- a/solution.py
+++ b/solution.py
@@ -17,7 +17,10 @@
 BF16 = jnp.bfloat16
 Z_ORDER = (4, 3, 5, 2, 6, 1, 7)
 ARRIVE = (1, 7, 2, 6, 3, 5, 4)
-RELAYED = 0
+HALF = NX // 2
+HALVES = SEC // 2
+NEAR = (1, 7, 2, 6)
+FAR = (3, 5, 4)
 
 
 def split(a):
@@ -47,8 +50,8 @@
     a_hbm, b_hbm, q_hbm, r_hbm, d_hbm, t_hbm, i_hbm,
     h_ref, grad_ref,
     a_v, b_v, q_v, r_v, d_v, t_v, i_v,
-    y_v, qy_v, x_tc, x_lr, z_tc, z_l, z_r, coef_a, coef_b, rhs,
-    in_sem, xt_s, xt_r, xl_s, xl_r, zt_s, zt_r, zl_s, zl_r, zr_s, zr_r, w_s, w_r,
+    y_v, qy_v, x_tc, x_lr, z_tc, z_f, z_l, z_r, coef_a, coef_b, rhs, fac,
+    in_sem, xt_s, xt_r, xl_s, xl_r, zt_s, zt_r, zl_s, zl_r, zf_s, zf_r, zr_s, zr_r, w_s, w_r,
 ):
     me = lax.axis_index("horizon")
     z, x = me // GX, me % GX
@@ -78,9 +81,9 @@
     for d in range(1, GZ):
         pl.semaphore_signal(barrier, inc=1, device_id={"horizon": z_peer(d)}, device_id_type=pl.DeviceIdType.MESH)
 
-    def remote(ref, send, recv, peer):
+    def remote(ref, send, recv, peer, into=None):
         return pltpu.make_async_remote_copy(
-            src_ref=ref, dst_ref=ref, send_sem=send, recv_sem=recv,
+            src_ref=ref, dst_ref=ref if into is None else into, send_sem=send, recv_sem=recv,
             device_id={"horizon": peer}, device_id_type=pl.DeviceIdType.MESH,
         )
 
@@ -108,16 +111,24 @@
     controls = jnp.transpose(
         jnp.concatenate([b_v[...].reshape(COLS, NX), jnp.zeros((COLS, 128 - NX), F32)], axis=1)
     )[:NX]
-    state = None
+    def added(t):
+        return jnp.concatenate([vector_at(t), jnp.where(lane // NU == t, controls, 0.0)], axis=1)
+
+    def first(t):
+        return added(t) + jnp.concatenate([a_v[t], wide, jnp.zeros((NX, 128), F32)], axis=1)
+
+    early, late = [first(0)], [first(HALVES)]
+    for t in range(1, HALVES):
+        early.append(mm(a_v[t], early[-1]) + added(t))
+        late.append(mm(a_v[HALVES + t], late[-1]) + added(HALVES + t))
+    joined = mm(jnp.concatenate([sq(v) for v in late], axis=0), early[-1])
+    narrow = jnp.concatenate([lane, lane + 128], axis=1) < NX
+    states = early + [
+        joined[NX * t : NX * (t + 1)] + jnp.where(narrow, 0.0, late[t]) for t in range(HALVES)
+    ]
+    state = states[-1]
     for t in range(SEC):
-        entry = vector_at(t)
-        placed = jnp.where(lane // NU == t, controls, 0.0)
-        added = jnp.concatenate([entry, placed], axis=1)
-        if t == 0:
-            state = added + jnp.concatenate([a_v[0], wide, jnp.zeros((NX, 128), F32)], axis=1)
-        else:
-            state = mm(a_v[t], state) + added
-        error = jnp.concatenate([state[:, :128] - vector_at(SEC + t), state[:, 128:]], axis=1)
+        error = jnp.concatenate([states[t][:, :128] - vector_at(SEC + t), states[t][:, 128:]], axis=1)
         y_v[NX * t : NX * (t + 1), :] = error
         qy_v[NX * t : NX * (t + 1), :] = mm(q_v[t], error)
     gram = mm(jnp.transpose(y_v[...]), qy_v[...])
@@ -131,13 +142,15 @@
     pl.semaphore_wait(barrier, GX - 1 + GZ - 1)
     sends = []
 
-    def send(ref, s, r, peer):
-        copy = remote(ref, s, r, peer)
+    def send(ref, s, r, peer, into=None):
+        copy = remote(ref, s, r, peer, into)
         copy.start()
         sends.append(copy)
 
     for d in (2, 1, 3):
         send(x_tc.at[x], xt_s.at[d], xt_r.at[x], x_peer(d))
+    for d in Z_ORDER:
+        send(x_lr.at[x, 0], zl_s.at[d], zl_r.at[z], z_peer(d), z_l.at[z])
     for d in (2, 1, 3):
         send(x_lr.at[x], xl_s.at[d], xl_r.at[x], x_peer(d))
 
@@ -192,16 +205,53 @@
     for d in Z_ORDER:
         send(z_tc.at[z], zt_s.at[d], zt_r.at[z], z_peer(d))
 
-    group_l = mm(sq(choose(x, after)), own_l)
+    follow = jnp.where(lane < NX, choose(x, after), 0.0)
+    z_f[z] = follow[:HALF] + pltpu.roll(follow[HALF:], 64, 1)
+    group_l = mm(sq(follow), own_l)
     group_r = mm(sq(choose(x, backs[:GX])), own_r) + mm(sq(choose(x, tails)), own_l)
-    z_l[z] = group_l
     z_r[z] = group_r
     for d in ARRIVE:
-        send(z_l.at[z], zl_s.at[d], zl_r.at[z], z_peer(d))
-    for d in ARRIVE:
+        send(z_f.at[z], zf_s.at[d], zf_r.at[z], z_peer(d))
+
         @pl.when((z + d) % GZ < z)
         def _():
             remote(z_r.at[z], zr_s.at[d], zr_r.at[z], z_peer(d)).start()
+
+    for d in range(1, GX):
+        i = (x + d) % GX
+        remote(x_lr.at[i], xl_s.at[d], xl_r.at[i], x_peer(d)).wait_recv()
+    own_follow = choose(x, after)
+    ups = [unit]
+    gains = []
+    for i in range(GX):
+        both = mm(sq(ups[i]), mixed(xp[i], xf[i]))
+        gains.append(jnp.where(i > x, cost_of(both), 0.0))
+        ups.append(jnp.where(lane < NX, jnp.where(i > x, both, unit), 0.0))
+    downs = [None] * GX
+    downs[GX - 1] = nothing
+    for i in reversed(range(1, GX)):
+        moved = mm(sq(downs[i]), xm[i]) + at_column(downs[i]) + gains[i]
+        downs[i - 1] = jnp.where(i == x, unit, moved)
+    near_tail = choose(x, downs)
+    to_exit = sq(ups[GX])
+    base, carried = [], []
+    for i in range(GX):
+        ca = jnp.where(i > x, ups[i], nothing)
+        base.append(mm(sq(ca), x_lr[i, 1]) + mm(sq(downs[i]), x_lr[i, 0]))
+        carried.append(jnp.where(i >= x, mm(sq(after[i]), x_lr[i, 0]), 0.0))
+    before = [unit, xm[0]]
+    for i in range(1, GX):
+        before.append(mm(sq(xm[i]), before[i]) + at_column(xm[i]))
+    reach = jnp.concatenate([choose(x, before[:GX]), choose(x, before[1:])], axis=0)
+    own_mt = choose(x, xf)[:NX]
+
+    def factors(value):
+        high, low = split(value)
+        stacked = jnp.concatenate([high.astype(F32), low.astype(F32), jnp.zeros((32, 128), F32)], axis=0)
+        return jnp.transpose(stacked).astype(BF16)
+
+    fac[1] = factors(group_l)
+    fac[3] = factors(own_l)
 
     for d in range(1, GZ):
         g = (z + d) % GZ
@@ -232,73 +282,55 @@
         coef_b[g] = downs[g]
     group_tail = choose(z, downs)
 
-    def forward(k):
-        g = (z + ARRIVE[k]) % GZ
-        i = (x + 1) % GX
-        remote(rhs.at[g, i], w_s.at[ARRIVE[k], 1], w_r.at[g, i], x_peer(1)).wait_recv()
-        send(rhs.at[g, i], w_s.at[ARRIVE[k], 2], w_r.at[g, i], x_peer(3))
-
-    for k, d in enumerate(ARRIVE):
-        g = (z + d) % GZ
-        remote(z_l.at[g], zl_s.at[d], zl_r.at[g], z_peer(d)).wait_recv()
-
-        @pl.when(g > z)
-        def _():
-            remote(z_r.at[g], zr_s.at[d], zr_r.at[g], z_peer(d)).wait_recv()
-
-        rhs[g, x] = mm(sq(coef_a[g]), z_r[g]) + mm(sq(coef_b[g]), z_l[g])
-        if k >= RELAYED:
-            send(rhs.at[g, x], w_s.at[d, 2], w_r.at[g, x], x_peer(2))
-        for e in (3, 1):
-            send(rhs.at[g, x], w_s.at[d, e], w_r.at[g, x], x_peer(e))
-        if 2 <= k < RELAYED + 2:
-            forward(k - 2)
-
-    for d in range(1, GX):
-        i = (x + d) % GX
-        remote(x_lr.at[i], xl_s.at[d], xl_r.at[i], x_peer(d)).wait_recv()
-    ups = [unit]
-    gains = []
-    for i in range(GX):
-        both = mm(sq(ups[i]), mixed(xp[i], xf[i]))
-        gains.append(jnp.where(i > x, cost_of(both), 0.0))
-        ups.append(jnp.where(lane < NX, jnp.where(i > x, both, unit), 0.0))
-    downs = [None] * GX
-    downs[GX - 1] = mm(sq(ups[GX]), group_tail)
-    for i in reversed(range(1, GX)):
-        moved = mm(sq(downs[i]), xm[i]) + at_column(downs[i]) + gains[i]
-        downs[i - 1] = jnp.where(i == x, unit, moved)
-    own_tail = choose(x, downs)
-    for i in range(GX):
-        ca = jnp.where(i > x, ups[i], nothing)
-        rhs[z, i] = mm(sq(ca), x_lr[i, 1]) + mm(sq(downs[i]), x_lr[i, 0])
-
-    for i in range(GX - 1):
-        enter = jnp.where(i < x, mm(sq(xm[i]), enter) + at_column(xm[i]), enter)
-    leaving = mm(own_t, enter) + at_column(state[:, :128])
-    costate = mm(sq(own_tail), leaving) + at_column(own_tail)
+    def pieces(batch):
+        through = {}
+        for d in batch:
+            g = (z + d) % GZ
+            remote(z_l.at[g], zl_s.at[d], zl_r.at[g], z_peer(d)).wait_recv()
+            remote(z_f.at[g], zf_s.at[d], zf_r.at[g], z_peer(d)).wait_recv()
+            packed = z_f[g]
+            through[d] = mm(
+                sq(coef_b[g]), jnp.concatenate([packed, pltpu.roll(packed, 64, 1)], axis=0)
+            )
+
+            @pl.when(g > z)
+            def _():
+                remote(z_r.at[g], zr_s.at[d], zr_r.at[g], z_peer(d)).wait_recv()
+
+        for d in batch:
+            g = (z + d) % GZ
+            rhs[g, x] = mm(sq(coef_a[g]), z_r[g]) + mm(sq(through[d]), z_l[g])
+        for d in batch:
+            g = (z + d) % GZ
+            for e in (2, 3, 1):
+                send(rhs.at[g, x], w_s.at[d, e], w_r.at[g, x], x_peer(e))
+
+    for d in ARRIVE:
+        pieces((d,))
+
+    inner = mm(sq(group_tail), jnp.concatenate([own_follow] + carried, axis=1))
+    inner = jnp.concatenate([inner[:, :128] + at_column(group_tail), inner[:, 128:]], axis=1)
+    outer = mm(to_exit, inner)
+    own_tail = near_tail + outer[:, :128]
+    blocks = [base[i] + outer[:, 128 * (i + 1) : 128 * (i + 2)] for i in range(GX)]
+    full_r = own_r + mm(sq(own_mt), choose(x, blocks))
+    group_mt = choose(z, zf)[:NX]
+    group_full = group_r + mm(
+        sq(group_mt), choose(x, [inner[:, 128 * (i + 1) : 128 * (i + 2)] for i in range(GX)])
+    )
+    fac[0] = factors(group_full)
+    fac[2] = factors(full_r)
+    both = mm(sq(reach), enter) + jnp.where(
+        jnp.concatenate([lane, lane], axis=0) == NX, reach, 0.0
+    )
+    costate = mm(sq(own_tail), both[NX:]) + at_column(own_tail)
     grad_ref[...] = gram[NX : NX + 1, 128:] + jnp.sum(
-        enter[:, NX : NX + 1] * own_r + costate[:, NX : NX + 1] * own_l, axis=0, keepdims=True
-    )
-
-    own_mt = choose(x, xf)[:NX]
-    full_r = own_r + mm(sq(own_mt), mm(sq(own_tail), own_l))
-    group_mt = choose(z, zf)[:NX]
-    group_full = group_r + mm(sq(group_mt), mm(sq(group_tail), group_l))
-
-    def factors(value):
-        high, low = split(value)
-        turned = jnp.transpose(
-            jnp.concatenate([high.astype(F32), low.astype(F32), jnp.zeros((32, 128), F32)], axis=0)
-        )
-        return turned.astype(BF16)[:, : 2 * NX]
+        both[:NX, NX : NX + 1] * own_r + costate[:, NX : NX + 1] * own_l, axis=0, keepdims=True
+    )
 
     def rows(left, right):
         high, low = split(right)
-        return dot(left, jnp.concatenate([high, high], axis=0)) + dot(left[:, :NX], low)
-
-    f_gl, f_gr = factors(group_l), factors(group_full)
-    f_l, f_r = factors(own_l), factors(full_r)
+        return dot(left[:, : 2 * NX], jnp.concatenate([high, high], axis=0)) + dot(left[:, :NX], low)
 
     tile = gram[128:, 128:]
     cost = jnp.concatenate(
@@ -311,20 +343,22 @@
         axis=0,
     )
     for i in range(GX):
-        left = jnp.where(i < x, f_r.astype(F32), f_l.astype(F32)).astype(BF16)
-        block = rows(left, rhs[z, i])
+        block = rows(fac[jnp.where(i < x, 2, 3)], blocks[i])
         block = block + jnp.where(i == x, tile + cost, 0.0)
         h_ref[:, pl.ds(pl.multiple_of(z * (GX * COLS) + i * COLS, COLS), COLS)] = block
 
-    for k, d in enumerate(ARRIVE):
-        g = (z + d) % GZ
-        left = jnp.where(g > z, f_gl.astype(F32), f_gr.astype(F32)).astype(BF16)
-        for e in range(1, GX):
-            i = (x + e) % GX
-            if k >= RELAYED or e != 1:
+    for batch in [(d,) for d in ARRIVE]:
+        for d in batch:
+            g = (z + d) % GZ
+            for e in range(1, GX):
+                i = (x + e) % GX
                 remote(rhs.at[g, i], w_s.at[d, e], w_r.at[g, i], x_peer(e)).wait_recv()
-        right = jnp.concatenate([rhs[g, i] for i in range(GX)], axis=1)
-        h_ref[:, pl.ds(pl.multiple_of(g * (GX * COLS), GX * COLS), GX * COLS)] = rows(left, right)
+        for d in batch:
+            g = (z + d) % GZ
+            right = jnp.concatenate([rhs[g, i] for i in range(GX)], axis=1)
+            h_ref[:, pl.ds(pl.multiple_of(g * (GX * COLS), GX * COLS), GX * COLS)] = rows(
+                fac[jnp.where(g > z, 1, 0)], right
+            )
 
     for copy in sends:
         copy.wait_send()
@@ -360,14 +394,16 @@
             pltpu.VMEM((GX, NX, 128), F32),
             pltpu.VMEM((GX, 2, NX, COLS), F32),
             pltpu.VMEM((GZ, NX, 128), F32),
+            pltpu.VMEM((GZ, HALF, 128), F32),
             pltpu.VMEM((GZ, NX, COLS), F32),
             pltpu.VMEM((GZ, NX, COLS), F32),
             pltpu.VMEM((GZ, NX, 128), F32),
             pltpu.VMEM((GZ, NX, 128), F32),
             pltpu.VMEM((GZ, GX, NX, COLS), F32),
+            pltpu.VMEM((4, 128, 128), BF16),
             dma((7,)),
             dma((GX,)), dma((GX,)), dma((GX,)), dma((GX,)),
-            dma((GZ,)), dma((GZ,)), dma((GZ,)), dma((GZ,)), dma((GZ,)), dma((GZ,)),
+            dma((GZ,)), dma((GZ,)), dma((GZ,)), dma((GZ,)), dma((GZ,)), dma((GZ,)), dma((GZ,)), dma((GZ,)),
             dma((GZ, GX)), dma((GZ, GX)),
         ],
         compiler_params=pltpu.CompilerParams(

time: 37.4 us -> 35 us (0.936)
  Pallas kernels: 34.8 us -> 32.4 us
    pallas_call x1, Pallas kernels: 34.8 us -> 32.4 us  [condense(): pl.pallas_call(body, out_shape=(jax.ShapeDtypeStruct((COLS, GX * GZ * COL...]
where the time goes in v3:
time: 35 us; the launch traced here: 34.9 us
  Pallas kernels  32.4 us (93%)
  local copies, waits for them, and re-layouts  1.83 us (5%)
  between operations  0.64 us (2%)
    pallas_call x1, Pallas kernels, condense(): pl.pallas_call(body, out_shape=(jax.ShapeDtypeStruct((COLS, GX * GZ * COL...  32.4 us
    unnamed x2, local copies, waits for them, and re-layouts  1.83 us

profile of v3, /device:TPU:8, one launch (start us, length us, event | category | flops | bytes accessed | tf_op | source)
XLA Modules:
  0.0 34.9 jit_solution(18363033337098267032)
XLA Ops:
  0.6 32.4 %condense.1 = (f32[128,4096]{1,0:T(8,128)S(1)}, f32[1,128]{1,0:T(1,128)S(1)}) custom-call(f32[1,8,48,48]{3,2,1,0:T(8,128)} %a_hbm.1, f32[1,8,16,48]{3,2,1,0:T(8,128)} %bitcast.3, f32[1,8,48,48]{3,2,1,0:T(8,128)} %q_hbm.1, f32[1,8,16,16]{3,2,1,0:T(8,128)} %r_hbm.1, f32[1,8,48]{2,1,0:T(8,128)} %d_hbm.1, f32[1,8,48]{2,1,0:T(8,128)} %t_hbm.1, f32[1,48]{1,0:T(1,128)} %i_hbm.1), custom_call_target="tpu_custom_call" | custom-call | tf_op jit(solution)/shard_map/condense/pallas_call | solution.py:373
  33.1 1.3 %copy.11 = f32[1,128,4096]{2,1,0:T(8,128)} copy(f32[1,128,4096]{2,1,0:T(8,128)S(1)} %bitcast.2) | data formatting | bytes 4194304
  34.4 0.5 %copy.12 = f32[1,128]{1,0:T(1,128)} copy(f32[1,128]{1,0:T(1,128)S(1)} %get-tuple-element.9) | data formatting | bytes 1024

commit v4 on v3

--- a/solution.py
+++ b/solution.py
@@ -19,6 +19,7 @@
 ARRIVE = (1, 7, 2, 6, 3, 5, 4)
 HALF = NX // 2
 HALVES = SEC // 2
+SPLITS = 4
 NEAR = (1, 7, 2, 6)
 FAR = (3, 5, 4)
 
@@ -35,7 +36,9 @@
 def mm(a, b):
     ah, al = split(a)
     bh, bl = split(b)
-    return dot(ah, bh) + (dot(ah, bl) + dot(al, bh))
+    n = a.shape[0]
+    both = dot(jnp.concatenate([ah, al], axis=0), bh)
+    return both[:n] + (dot(ah, bl) + both[n:])
 
 
 def sq(a):
@@ -87,8 +90,8 @@
             device_id={"horizon": peer}, device_id_type=pl.DeviceIdType.MESH,
         )
 
-    for load in loads:
-        load.wait()
+    for k in (0, 1, 2, 3, 6):
+        loads[k].wait()
 
     lane = lax.broadcasted_iota(jnp.int32, (NX, 128), 1)
     row = lax.broadcasted_iota(jnp.int32, (NX, 128), 0)
@@ -127,6 +130,7 @@
         joined[NX * t : NX * (t + 1)] + jnp.where(narrow, 0.0, late[t]) for t in range(HALVES)
     ]
     state = states[-1]
+    loads[4].wait()
     for t in range(SEC):
         error = jnp.concatenate([states[t][:, :128] - vector_at(SEC + t), states[t][:, 128:]], axis=1)
         y_v[NX * t : NX * (t + 1), :] = error
@@ -184,31 +188,29 @@
     xp = [x_tc[i] for i in range(GX)]
     xf = [turned(p) for p in xp]
     xm = [maps_of(p) for p in xp]
-    backs = [unit, jnp.where(lane < NX, xf[0][:NX], 0.0)]
-    gains = [cost_of(xp[0])]
-    for i in range(1, GX):
-        both = mm(sq(backs[i]), mixed(xp[i], xf[i]))
-        backs.append(both)
-        gains.append(cost_of(both))
-    tails = [None] * GX
-    after = [None] * GX
-    tails[GX - 1], after[GX - 1] = nothing, unit
-    tails[GX - 2], after[GX - 2] = gains[GX - 1], xm[GX - 1]
-    for i in reversed(range(GX - 1)):
-        stack = mm(sq(jnp.concatenate([tails[i], after[i]], axis=0)), xm[i])
-        low = stack[:NX] + at_column(tails[i]) + gains[i]
-        high = stack[NX:] + at_column(after[i])
-        if i:
-            tails[i - 1], after[i - 1] = low, high
-    group_cost, group_map = low, high
+    first_back = jnp.where(lane < NX, xf[0][:NX], 0.0)
+    one = mm(sq(first_back), mixed(xp[1], xf[1]))
+    three = mm(xf[2][:NX, :NX], mixed(xp[3], xf[3]))
+    gain_one, gain_three = cost_of(one), cost_of(three)
+    low_cost = cost_of(xp[0]) + mm(sq(gain_one), xm[0]) + at_column(gain_one)
+    high_cost = cost_of(xp[2]) + mm(sq(gain_three), xm[2]) + at_column(gain_three)
+    low_map = mm(sq(xm[1]), xm[0]) + at_column(xm[1])
+    high_map = mm(sq(xm[3]), xm[2]) + at_column(xm[3])
+    low_back = jnp.where(lane < NX, one, 0.0)
+    gain_high = mm(sq(low_back), high_cost)
+    group_cost = low_cost + mm(sq(gain_high), low_map) + at_column(gain_high)
+    group_map = mm(sq(high_map), low_map) + at_column(high_map)
     z_tc[z] = group_map + pltpu.roll(group_cost, 64, 1)
     for d in Z_ORDER:
         send(z_tc.at[z], zt_s.at[d], zt_r.at[z], z_peer(d))
 
+    after = [mm(sq(high_map), xm[1]) + at_column(high_map), high_map, xm[3], unit]
     follow = jnp.where(lane < NX, choose(x, after), 0.0)
     z_f[z] = follow[:HALF] + pltpu.roll(follow[HALF:], 64, 1)
+    backs = [unit, first_back, low_back, mm(sq(low_back), xf[2][:NX])]
+    tails = [gain_one + mm(sq(gain_high), xm[1]), gain_high, mm(sq(backs[3]), cost_of(xp[3])), nothing]
     group_l = mm(sq(follow), own_l)
-    group_r = mm(sq(choose(x, backs[:GX])), own_r) + mm(sq(choose(x, tails)), own_l)
+    group_r = mm(sq(choose(x, backs)), own_r) + mm(sq(choose(x, tails)), own_l)
     z_r[z] = group_r
     for d in ARRIVE:
         send(z_f.at[z], zf_s.at[d], zf_r.at[z], z_peer(d))
@@ -239,9 +241,7 @@
         ca = jnp.where(i > x, ups[i], nothing)
         base.append(mm(sq(ca), x_lr[i, 1]) + mm(sq(downs[i]), x_lr[i, 0]))
         carried.append(jnp.where(i >= x, mm(sq(after[i]), x_lr[i, 0]), 0.0))
-    before = [unit, xm[0]]
-    for i in range(1, GX):
-        before.append(mm(sq(xm[i]), before[i]) + at_column(xm[i]))
+    before = [unit, xm[0], low_map, mm(sq(xm[2]), low_map) + at_column(xm[2]), group_map]
     reach = jnp.concatenate([choose(x, before[:GX]), choose(x, before[1:])], axis=0)
     own_mt = choose(x, xf)[:NX]
 
@@ -332,6 +332,7 @@
         high, low = split(right)
         return dot(left[:, : 2 * NX], jnp.concatenate([high, high], axis=0)) + dot(left[:, :NX], low)
 
+    loads[5].wait()
     tile = gram[128:, 128:]
     cost = jnp.concatenate(
         [
@@ -366,6 +367,18 @@
         @pl.when((z + d) % GZ < z)
         def _():
             remote(z_r.at[z], zr_s.at[d], zr_r.at[z], z_peer(d)).wait_send()
+
+
+def settle(h_v, g_v, h_out, g_out, sem):
+    size = COLS // SPLITS
+    copies = [pltpu.make_async_copy(g_v, g_out, sem.at[SPLITS])]
+    for k in range(SPLITS):
+        part = pl.ds(size * k, size)
+        copies.append(pltpu.make_async_copy(h_v.at[part], h_out.at[0, part], sem.at[k]))
+    for copy in copies:
+        copy.start()
+    for copy in copies:
+        copy.wait()
 
 
 def condense(dynamics, inputs, state_cost, input_cost, drift, target, initial):
@@ -411,7 +424,18 @@
         ),
         name="condense",
     )(*(pltpu.with_memory_space_constraint(v, pltpu.HBM) for v in (dynamics, jnp.swapaxes(inputs, 2, 3), state_cost, input_cost, drift, target, initial)))
-    return hessian[None], gradient
+    return pl.pallas_call(
+        settle,
+        out_shape=(
+            jax.ShapeDtypeStruct((1, COLS, GX * GZ * COLS), F32),
+            jax.ShapeDtypeStruct((1, COLS), F32),
+        ),
+        in_specs=[pl.BlockSpec(memory_space=pltpu.VMEM)] * 2,
+        out_specs=(pl.BlockSpec(memory_space=pltpu.HBM), pl.BlockSpec(memory_space=pltpu.HBM)),
+        scratch_shapes=[dma((SPLITS + 1,))],
+        compiler_params=pltpu.CompilerParams(vmem_limit_bytes=4 * 1024 * 1024),
+        name="settle",
+    )(hessian, gradient)
 
 
 def solution(mesh):

time: 35 us -> 34.4 us (0.983)
  local copies, waits for them, and re-layouts: 1.83 us -> 0 us
  Pallas kernels: 32.4 us -> 33.7 us
    unnamed x2 -> x0, local copies, waits for them, and re-layouts: 1.83 us -> none
    pallas_call x0 -> x1, Pallas kernels: none -> 1.36 us  [condense(): pl.pallas_call(settle, out_shape=(jax.ShapeDtypeStruct((1, COLS, GX * GZ...]
where the time goes in v4:
time: 34.4 us; the launch traced here: 34.3 us
  Pallas kernels  33.7 us (98%)
  between operations  0.64 us (2%)
    pallas_call x1, Pallas kernels, condense(): pl.pallas_call(body, out_shape=(jax.ShapeDtypeStruct((COLS, GX * GZ * COL...  32.3 us
    pallas_call x1, Pallas kernels, condense(): pl.pallas_call(settle, out_shape=(jax.ShapeDtypeStruct((1, COLS, GX * GZ...  1.36 us

profile of v4, /device:TPU:8, one launch (start us, length us, event | category | flops | bytes accessed | tf_op | source)
XLA Modules:
  0.0 34.3 jit_solution(8071791275838308443)
XLA Ops:
  0.6 32.3 %condense.1 = (f32[128,4096]{1,0:T(8,128)S(1)}, f32[1,128]{1,0:T(1,128)S(1)}) custom-call(f32[1,8,48,48]{3,2,1,0:T(8,128)} %a_hbm.1, f32[1,8,16,48]{3,2,1,0:T(8,128)} %bitcast.1, f32[1,8,48,48]{3,2,1,0:T(8,128)} %q_hbm.1, f32[1,8,16,16]{3,2,1,0:T(8,128)} %r_hbm.1, f32[1,8,48]{2,1,0:T(8,128)} %d_hbm.1, f32[1,8,48]{2,1,0:T(8,128)} %t_hbm.1, f32[1,48]{1,0:T(1,128)} %i_hbm.1), custom_call_target="tpu_custom_call" | custom-call | tf_op jit(solution)/shard_map/condense/pallas_call | solution.py:386
  33.0 1.4 %settle.1 = (f32[1,128,4096]{2,1,0:T(8,128)}, f32[1,128]{1,0:T(1,128)}) custom-call(f32[128,4096]{1,0:T(8,128)S(1)} %get-tuple-element.4.h_v, f32[1,128]{1,0:T(1,128)S(1)} %get-tuple-element.5.g_v), custom_call_target="tpu_custom_call" | custom-call | tf_op jit(solution)/shard_map/settle/pallas_call | solution.py:427

commit v5 on v4

--- a/solution.py
+++ b/solution.py
@@ -16,10 +16,10 @@
 F32 = jnp.float32
 BF16 = jnp.bfloat16
 Z_ORDER = (4, 3, 5, 2, 6, 1, 7)
-ARRIVE = (1, 7, 2, 6, 3, 5, 4)
+ARRIVE = (1, 7, 2, 6, 5, 3, 4)
+SENDS = (7, 1, 6, 2, 3, 5, 4)
 HALF = NX // 2
 HALVES = SEC // 2
-SPLITS = 4
 NEAR = (1, 7, 2, 6)
 FAR = (3, 5, 4)
 
@@ -41,6 +41,11 @@
     return both[:n] + (dot(ah, bl) + both[n:])
 
 
+def rows(left, right):
+    high, low = split(right)
+    return dot(left[:, : 2 * NX], jnp.concatenate([high, high], axis=0)) + dot(left[:, :NX], low)
+
+
 def sq(a):
     return a[:, :NX]
 
@@ -51,7 +56,7 @@
 
 def body(
     a_hbm, b_hbm, q_hbm, r_hbm, d_hbm, t_hbm, i_hbm,
-    h_ref, grad_ref,
+    h_ref, grad_ref, right_ref, left_ref,
     a_v, b_v, q_v, r_v, d_v, t_v, i_v,
     y_v, qy_v, x_tc, x_lr, z_tc, z_f, z_l, z_r, coef_a, coef_b, rhs, fac,
     in_sem, xt_s, xt_r, xl_s, xl_r, zt_s, zt_r, zl_s, zl_r, zf_s, zf_r, zr_s, zr_r, w_s, w_r,
@@ -212,7 +217,7 @@
     group_l = mm(sq(follow), own_l)
     group_r = mm(sq(choose(x, backs)), own_r) + mm(sq(choose(x, tails)), own_l)
     z_r[z] = group_r
-    for d in ARRIVE:
+    for d in SENDS:
         send(z_f.at[z], zf_s.at[d], zf_r.at[z], z_peer(d))
 
         @pl.when((z + d) % GZ < z)
@@ -328,10 +333,6 @@
         both[:NX, NX : NX + 1] * own_r + costate[:, NX : NX + 1] * own_l, axis=0, keepdims=True
     )
 
-    def rows(left, right):
-        high, low = split(right)
-        return dot(left[:, : 2 * NX], jnp.concatenate([high, high], axis=0)) + dot(left[:, :NX], low)
-
     loads[5].wait()
     tile = gram[128:, 128:]
     cost = jnp.concatenate(
@@ -357,6 +358,10 @@
         for d in batch:
             g = (z + d) % GZ
             right = jnp.concatenate([rhs[g, i] for i in range(GX)], axis=1)
+            if d == ARRIVE[-1]:
+                right_ref[...] = right
+                left_ref[...] = fac[jnp.where(g > z, 1, 0)].astype(F32)
+                continue
             h_ref[:, pl.ds(pl.multiple_of(g * (GX * COLS), GX * COLS), GX * COLS)] = rows(
                 fac[jnp.where(g > z, 1, 0)], right
             )
@@ -369,31 +374,39 @@
             remote(z_r.at[z], zr_s.at[d], zr_r.at[z], z_peer(d)).wait_send()
 
 
-def settle(h_v, g_v, h_out, g_out, sem):
-    size = COLS // SPLITS
-    copies = [pltpu.make_async_copy(g_v, g_out, sem.at[SPLITS])]
-    for k in range(SPLITS):
-        part = pl.ds(size * k, size)
-        copies.append(pltpu.make_async_copy(h_v.at[part], h_out.at[0, part], sem.at[k]))
+def settle(h_v, g_v, right_v, left_v, h_out, g_out, last, sem):
+    z = lax.axis_index("horizon") // GX
+    wide = GX * COLS
+
+    def columns(d):
+        return pl.ds(pl.multiple_of(((z + d) % GZ) * wide, wide), wide)
+
+    copies = []
+    for d in range(GZ):
+        if d != ARRIVE[-1]:
+            copies.append(pltpu.make_async_copy(h_v.at[:, columns(d)], h_out.at[0, :, columns(d)], sem.at[d]))
+    copies.append(pltpu.make_async_copy(g_v, g_out, sem.at[GZ]))
     for copy in copies:
         copy.start()
+    last[...] = rows(left_v[...].astype(BF16), right_v[...])
+    copies.append(pltpu.make_async_copy(last, h_out.at[0, :, columns(ARRIVE[-1])], sem.at[ARRIVE[-1]]))
+    copies[-1].start()
     for copy in copies:
         copy.wait()
 
 
 def condense(dynamics, inputs, state_cost, input_cost, drift, target, initial):
     dma = pltpu.SemaphoreType.DMA
-    hessian, gradient = pl.pallas_call(
+    results = pl.pallas_call(
         body,
         out_shape=(
             jax.ShapeDtypeStruct((COLS, GX * GZ * COLS), F32),
             jax.ShapeDtypeStruct((1, COLS), F32),
+            jax.ShapeDtypeStruct((NX, GX * COLS), F32),
+            jax.ShapeDtypeStruct((COLS, 128), F32),
         ),
         in_specs=[pl.BlockSpec(memory_space=pltpu.HBM)] * 7,
-        out_specs=(
-            pl.BlockSpec(memory_space=pltpu.VMEM),
-            pl.BlockSpec(memory_space=pltpu.VMEM),
-        ),
+        out_specs=(pl.BlockSpec(memory_space=pltpu.VMEM),) * 4,
         scratch_shapes=[
             pltpu.VMEM((SEC, NX, NX), F32),
             pltpu.VMEM((SEC, NU, NX), F32),
@@ -430,12 +443,12 @@
             jax.ShapeDtypeStruct((1, COLS, GX * GZ * COLS), F32),
             jax.ShapeDtypeStruct((1, COLS), F32),
         ),
-        in_specs=[pl.BlockSpec(memory_space=pltpu.VMEM)] * 2,
+        in_specs=[pl.BlockSpec(memory_space=pltpu.VMEM)] * 4,
         out_specs=(pl.BlockSpec(memory_space=pltpu.HBM), pl.BlockSpec(memory_space=pltpu.HBM)),
-        scratch_shapes=[dma((SPLITS + 1,))],
+        scratch_shapes=[pltpu.VMEM((COLS, GX * COLS), F32), dma((GZ + 1,))],
         compiler_params=pltpu.CompilerParams(vmem_limit_bytes=4 * 1024 * 1024),
         name="settle",
-    )(hessian, gradient)
+    )(*results)
 
 
 def solution(mesh):

time: 34.4 us -> 34.3 us (level)
  no operation moved by 1% of the time
where the time goes in v5:
time: 34.3 us; the launch traced here: 34.2 us
  Pallas kernels  33.6 us (98%)
  between operations  0.64 us (2%)
    pallas_call x1, Pallas kernels, condense(): pl.pallas_call(body, out_shape=(jax.ShapeDtypeStruct((COLS, GX * GZ * COL...  32.1 us
    pallas_call x1, Pallas kernels, condense(): pl.pallas_call(settle, out_shape=(jax.ShapeDtypeStruct((1, COLS, GX * GZ...  1.44 us

profile of v5, /device:TPU:8, one launch (start us, length us, event | category | flops | bytes accessed | tf_op | source)
XLA Modules:
  0.0 34.2 jit_solution(3597544267937526628)
XLA Ops:
  0.6 32.1 %condense.1 = (f32[128,4096]{1,0:T(8,128)S(1)}, f32[1,128]{1,0:T(1,128)S(1)}, f32[48,512]{1,0:T(8,128)S(1)}, f32[128,128]{1,0:T(8,128)S(1)}) custom-call(f32[1,8,48,48]{3,2,1,0:T(8,128)} %a_hbm.1, f32[1,8,16,48]{3,2,1,0:T(8,128)} %bitcast.1, f32[1,8,48,48]{3,2,1,0:T(8,128)} %q_hbm.1, f32[1,8,16,16]{3,2,1,0:T(8,128)} %r_hbm.1, f32[1,8,48]{2,1,0:T(8,128)} %d_hbm.1, ...), custom_call_target="tpu_custom_call" | custom-call | tf_op jit(solution)/shard_map/condense/pallas_call | solution.py:400
  32.8 1.4 %settle.1 = (f32[1,128,4096]{2,1,0:T(8,128)}, f32[1,128]{1,0:T(1,128)}) custom-call(f32[128,4096]{1,0:T(8,128)S(1)} %get-tuple-element.6.h_v, f32[1,128]{1,0:T(1,128)S(1)} %get-tuple-element.7.g_v, f32[48,512]{1,0:T(8,128)S(1)} %get-tuple-element.8.right_v, f32[128,128]{1,0:T(8,128)S(1)} %get-tuple-element.9.left_v), custom_call_target="tpu_custom_call" | custom-call | tf_op jit(solution)/shard_map/settle/pallas_call | solution.py:440
